TPU v7x, 256 devices: a whole 4x4x8 slice. The times are simulated.
256 devices in a mesh: paths: 8 (over x, core), cpty: 32 (over z, y).
Axes of the slice: x: 4, y: 4, z: 8, core: 2. Of those that a mesh axis runs over, the one named last changes fastest.
Arguments:
- factors: bfloat16 [64, 12288], P(None, 'paths'), may hold values from -6 to 6
- loadings: bfloat16 [64, 65536], P(None, 'cpty'), may hold values from -2 to 2
- notional: bfloat16 [65536], P('cpty'), may hold values from 0.25 to 0.796875
- strike: bfloat16 [65536], P('cpty'), may hold values from 2 to 8
- curvature: bfloat16 [65536], P('cpty'), may hold values from 1 to 3
- trade_cpty: int32 [65536], P('cpty'), may hold values from 0 to 4095, as said below
Outputs:
- exposure: bfloat16 [12288, 4096], P('paths', 'cpty')
- moment: float32 [4096, 4096], P('paths', 'cpty')
Inputs may be any that keep to these rules, and one draw needn't show every extreme that they name: `trade_cpty`: of the trades in the book of one index of cpty, at most 128 belong to the counterparties numbered k * 128 to (k + 1) * 128 - 1 for any k; in every draw some such k receives exactly 128 from every book.
All inputs are finite; a program needn't handle non-finite values.
Results may differ from a plain program's by a relative error of at most 0.0064.
Values may be sent and summed in bfloat16 or wider, within the bound.
A program may use at most 128 MiB of HBM per device.

v0:
```python
import jax
import jax.numpy as jnp
from jax import lax
from jax.sharding import PartitionSpec as P

CP_DEV = 128


def in_blocks(x, dim, length):
    before, after = (x.shape[:dim], x.shape[dim + 1 :])
    return jnp.moveaxis(x.reshape(*before, length, -1, *after), dim, 0)


def summed_on_arrival(x, axis, dim):
    parts = in_blocks(x, dim, lax.axis_size(axis))
    arrived = lax.all_to_all(parts, axis, split_axis=0, concat_axis=0, tiled=True)
    return arrived.astype(jnp.float32).sum(axis=0)


def price_trades(drivers, loading_cols, trade_terms):
    linear = jnp.dot(drivers, loading_cols, preferred_element_type=jnp.float32)
    terms_wide = trade_terms.astype(jnp.float32)
    value = terms_wide[0] * (linear + terms_wide[2] * jnp.tanh(linear - terms_wide[1]))
    return value.astype(jnp.bfloat16)


def on_device(factors, loadings, notional, strike, curvature, trade_cpty):
    groups = lax.axis_size("cpty")
    own_index = lax.axis_index("cpty")
    trades = loadings.shape[1]
    slot_size = 2 * trades // groups
    owners = trade_cpty // CP_DEV
    marked = (owners[:, None] == jnp.arange(groups, dtype=jnp.int32)[None, :]).astype(jnp.int32)
    ranking = jnp.sum((jnp.cumsum(marked, axis=0) - marked) * marked, axis=1)
    target = owners * slot_size + ranking
    chosen = (
        jnp.zeros((groups * slot_size,), jnp.int32)
        .at[target]
        .set(jnp.arange(trades, dtype=jnp.int32))
    )
    filled = jnp.zeros((groups * slot_size,), jnp.bool_).at[target].set(True)
    labels = jnp.where(filled, trade_cpty[chosen], -1)[None, :]
    drivers = jnp.transpose(factors)
    trade_terms = jnp.stack([notional, strike, curvature])
    described = jnp.concatenate([loadings, trade_terms], axis=0)
    packed = jnp.where(
        filled[None, :], jnp.take(described, chosen, axis=1), jnp.zeros((), jnp.bfloat16)
    )
    received, arrived_ids = (
        lax.all_to_all(packed, "cpty", split_axis=1, concat_axis=1, tiled=True),
        lax.all_to_all(labels, "cpty", split_axis=1, concat_axis=1, tiled=True),
    )
    factor_count = loadings.shape[0]
    arrived = price_trades(drivers, received[:factor_count], received[factor_count:])
    local_ids = arrived_ids[0] - own_index * CP_DEV
    onehot = (local_ids[:, None] == jnp.arange(CP_DEV, dtype=jnp.int32)[None, :]).astype(
        jnp.bfloat16
    )
    netted = jnp.dot(arrived, onehot, preferred_element_type=jnp.float32)
    exposure = jnp.maximum(netted, 0.0).astype(jnp.bfloat16)
    everyone = lax.all_gather(exposure, "cpty", axis=1, tiled=True)
    path_total = exposure.shape[0] * lax.axis_size("paths")
    moment = (
        summed_on_arrival(
            jnp.einsum("pa,pb->ab", everyone, exposure, preferred_element_type=jnp.float32).astype(
                jnp.bfloat16
            ),
            "paths",
            0,
        )
        / path_total
    )
    return (exposure, moment)


def solution(mesh):
    in_specs = (P(None, "paths"), P(None, "cpty"), P("cpty"), P("cpty"), P("cpty"), P("cpty"))
    out_specs = (P("paths", "cpty"), P("paths", "cpty"))
    return jax.shard_map(
        on_device, mesh=mesh, in_specs=in_specs, out_specs=out_specs, check_vma=False
    )
```

profile of v0, /device:TPU:4, one launch (start us, length us, event | category | flops | bytes accessed | tf_op | source)
XLA Modules:
  0.0 284.2 jit_solution(17059434159926769436)
XLA Ops:
  7.2 0.8 add_select_fusion
  8.0 9.1 %reduce-window.6 = s32[32,16,128]{2,1,0:T(8,128)S(1)} reduce-window(s32[32,16,128]{2,1,0:T(8,128)S(1)} %fusion.18, s32[]{:T(128)} %constant.24.clone.1), window={size=1x1x128 pad=0_0x0_0x127_0}, to_apply=%region_0.1 | reduce-window | flops 8323072 | bytes 524292 | tf_op jit(solution)/shard_map/reduce-window
  17.1 0.1 slice.40
  17.2 0.2 copy.33
  17.5 0.2 reduce-window.9
  17.7 0.1 broadcast_add_fusion
  17.8 0.1 fusion.17
  17.9 0.7 compare_select_fusion.1
  18.7 8.1 %scatter_custom_fusion.1 = s32[4096]{0:T(1024)S(1)} fusion(s32[2048]{0:T(1024)S(1)} %compare_select_fusion.1, s32[2048]{0:T(1024)S(1)} %iota.15, s32[]{:T(128)} %constant.24.clone.1), kind=kCustom, calls=%fused_computation.49 | custom fusion | bytes 16388 | tf_op jit(solution)/shard_map/scatter | solution.py:39
  26.7 23.0 %gather_fusion.1 = s32[4096]{0:T(1024)S(1)} fusion(s32[2048]{0:T(1024)S(1)} %copy-done.1, s32[4096]{0:T(1024)S(1)} %fusion.19), kind=kCustom, calls=%fused_computation.1 | custom fusion | bytes 49152 | tf_op jit(solution)/shard_map/gather | solution.py:42
  49.8 9.1 %scatter_custom_fusion = pred[4096]{0:T(1024)(128)(4,1)S(1)} fusion(s32[2048]{0:T(1024)S(1)} %compare_select_fusion.1, pred[2048]{0:T(1024)(128)(4,1)S(1)} %broadcast.49, pred[]{:T(512)} %constant.22.clone.1), kind=kCustom, calls=%fused_computation.53 | custom fusion | bytes 4097 | tf_op jit(solution)/shard_map/scatter | solution.py:41
  58.9 0.6 broadcast_select_fusion
  59.5 11.5 %all-to-all-start.1 = ((s32[1,32,128]{2,0,1:T(1,128)}), s32[1,32,128]{2,0,1:T(1,128)S(1)}, u32[]{:S(2)}, u32[]{:S(2)}) async-start(s32[1,32,128]{2,0,1:T(1,128)} %bitcast.12), calls=%async_computation.1 | async-start | bytes 32768 | tf_op jit(solution)/shard_map/all_to_all | solution.py:51
  71.1 0.3 copy.26
  71.4 0.3 stack.12
  71.7 0.3 stack.13
  72.1 0.3 stack.14
  72.4 0.7 pad_maximum_fusion
  73.1 12.1 %gather_fusion = bf16[4096,67]{1,0:T(8,128)(2,1)S(1)} fusion(bf16[67,2048]{0,1:T(8,128)(2,1)S(1)} %pad_maximum_fusion, s32[4096]{0:T(1024)S(1)} %fusion.19), kind=kCustom, calls=%fused_computation | custom fusion | bytes 1114112 | tf_op jit(solution)/shard_map/jit(_take)/gather | solution.py:47
  85.3 0.6 copy.30
  85.9 0.9 select_select_fusion
  86.8 9.8 %all-to-all-start = ((bf16[67,32,128]{2,0,1:T(8,128)(2,1)}), bf16[67,32,128]{2,0,1:T(8,128)(2,1)S(1)}, u32[]{:S(2)}, u32[]{:S(2)}) async-start(bf16[67,32,128]{2,0,1:T(8,128)(2,1)} %select_select_fusion), calls=%async_computation | async-start | bytes 1179648 | tf_op jit(solution)/shard_map/all_to_all | solution.py:50
  96.6 0.0 all-gather.2.cloned.1.call-start
  96.7 0.9 iota_compare_fusion.7
  97.6 17.5 %all-to-all-done = bf16[67,32,128]{2,0,1:T(8,128)(2,1)S(1)} async-done(((bf16[67,32,128]{2,0,1:T(8,128)(2,1)}), bf16[67,32,128]{2,0,1:T(8,128)(2,1)S(1)}, u32[]{:S(2)}, u32[]{:S(2)}) %all-to-all-start) | async-done | bytes 548896 | tf_op jit(solution)/shard_map/all_to_all | solution.py:50
  115.1 14.0 %fusion.9 = bf16[1536,128]{1,0:T(8,128)(2,1)} fusion(bf16[64,1536]{1,0:T(8,128)(2,1)S(1)} %copy-done, f32[4096]{0:T(1024)S(1)} %get-tuple-element.3, f32[4096]{0:T(1024)S(1)} %get-tuple-element.4, f32[4096]{0:T(1024)S(1)} %get-tuple-element.2, bf16[67,32,128]{2,0,1:T(8,128)(2,1)S(1)} %all-to-all-done, pred[4096,128]{1,0:T(32,128)(4,1)S(1)} %iota_compare_fusion.7), kind=kOutput, calls=%fused_computation.16 | convolution fusion | flops 2447769600 | bytes 1687552 | tf_op jit(solution)/shard_map/dot_general | solution.py:59
  129.1 0.0 all-gather.2.cloned.1.call-update
  129.1 121.8 %all-gather.2.cloned.1.call-done = bf16[1536,4096]{1,0:T(8,128)(2,1)} async-done(((bf16[1536,128]{1,0:T(8,128)(2,1)}), bf16[1536,4096]{1,0:T(8,128)(2,1)}) %all-gather.2.cloned.1.call-update) | async-done | bytes 12582928 | tf_op jit(solution)/shard_map/all_gather | solution.py:61
  250.9 8.1 %convolution_convert_fusion = bf16[4096,128]{1,0:T(8,128)(2,1)S(1)} fusion(bf16[1536,4096]{1,0:T(8,128)(2,1)} %all-gather.2.cloned.1.call-done, bf16[1536,128]{1,0:T(8,128)(2,1)} %fusion.9), kind=kOutput, calls=%fused_computation.14 | convolution fusion | flops 1611137024 | bytes 14024704 | tf_op jit(solution)/shard_map/pa,pb->ab/dot_general | solution.py:65
  259.0 17.5 %all_to_all.20 = bf16[8,512,128]{2,1,0:T(8,128)(2,1)S(1)} all-to-all(bf16[8,512,128]{2,1,0:T(8,128)(2,1)S(1)} %bitcast.86), channel_id=1, replica_groups=mesh['paths'=8,'cpty'=32] {'paths'}, dimensions={0} | all-to-all | bytes 2097152 | tf_op jit(solution)/shard_map/all_to_all | solution.py:16
  276.5 0.1 convert_reduce_fusion
  276.6 0.7 broadcast_multiply_fusion
  (22 shorter events, 0.1 us)
Async XLA Ops:
  7.2 107.9 %copy-start = (bf16[64,1536]{1,0:T(8,128)(2,1)S(1)}, bf16[64,1536]{1,0:T(8,128)(2,1)}, u32[]{:S(2)}) copy-start(bf16[64,1536]{1,0:T(8,128)(2,1)} %param.6) | copy-start | bytes 589828
  7.2 19.6 %copy-start.1 = (s32[2048]{0:T(1024)S(1)}, s32[2048]{0:T(1024)}, u32[]{:S(2)}) copy-start(s32[2048]{0:T(1024)} %param.11) | copy-start | bytes 24580
  7.2 63.9 %copy-start.2 = (bf16[64,2048]{1,0:T(8,128)(2,1)S(1)}, bf16[64,2048]{1,0:T(8,128)(2,1)}, u32[]{:S(2)}) copy-start(bf16[64,2048]{1,0:T(8,128)(2,1)} %param.7) | copy-start | bytes 786436
  7.2 64.2 %copy-start.3 = (bf16[2048]{0:T(1024)(128)(2,1)S(1)}, bf16[2048]{0:T(1024)(128)(2,1)}, u32[]{:S(2)}) copy-start(bf16[2048]{0:T(1024)(128)(2,1)} %param.8) | copy-start | bytes 12292
  7.2 64.5 %copy-start.4 = (bf16[2048]{0:T(1024)(128)(2,1)S(1)}, bf16[2048]{0:T(1024)(128)(2,1)}, u32[]{:S(2)}) copy-start(bf16[2048]{0:T(1024)(128)(2,1)} %param.9) | copy-start | bytes 12292
  7.2 64.8 %copy-start.5 = (bf16[2048]{0:T(1024)(128)(2,1)S(1)}, bf16[2048]{0:T(1024)(128)(2,1)}, u32[]{:S(2)}) copy-start(bf16[2048]{0:T(1024)(128)(2,1)} %param.10) | copy-start | bytes 12292
  59.5 27.3 %all-to-all-start.1 = ((s32[1,32,128]{2,0,1:T(1,128)}), s32[1,32,128]{2,0,1:T(1,128)S(1)}, u32[]{:S(2)}, u32[]{:S(2)}) async-start(s32[1,32,128]{2,0,1:T(1,128)} %bitcast.12), calls=%async_computation.1 | async-start | bytes 32768 | tf_op jit(solution)/shard_map/all_to_all | solution.py:51
  86.8 28.2 %all-to-all-start = ((bf16[67,32,128]{2,0,1:T(8,128)(2,1)}), bf16[67,32,128]{2,0,1:T(8,128)(2,1)S(1)}, u32[]{:S(2)}, u32[]{:S(2)}) async-start(bf16[67,32,128]{2,0,1:T(8,128)(2,1)} %select_select_fusion), calls=%async_computation | async-start | bytes 1179648 | tf_op jit(solution)/shard_map/all_to_all | solution.py:50
  96.6 154.3 %all-gather.2.cloned.1.call-start = ((), (), s32[]{:S(2)}) async-start(), calls=%async_computation.3 | async-start | bytes 12976128 | tf_op jit(solution)/shard_map/all_gather | solution.py:61
Sparse Core Ops, SparseCore 0:
  129.2 121.6 all-gather.1
where the time goes:
time: 288 us; the launch traced here: 284 us
  waiting for transfers between devices  139 us (48%)
  local copies, waits for them, and re-layouts  54.7 us (19%)
  matrix products  22.1 us (8%)
  starting transfers between devices  21.3 us (7%)
  blocking collectives  17.5 us (6%)
  other arithmetic  15 us (5%)
  between operations  14.3 us (5%)
    all_gather x1, waiting for transfers between devices, on_device(): everyone = lax.all_gather(exposure, 'cpty', axis=1, tiled=True)  122 us
    gather x1, local copies, waits for them, and re-layouts, on_device(): labels = jnp.where(filled, trade_cpty[chosen], -1)[None, :]  23 us
    all_to_all x1, blocking collectives, summed_on_arrival(): lax.all_to_all(parts, axis, split_axis=0, concat_axis=0, tiled=True)  17.5 us
    all_to_all x1, waiting for transfers between devices, on_device(): lax.all_to_all(packed, 'cpty', split_axis=1, concat_axis=1, tiled=True)  17.5 us
    dot_general x1, matrix products, on_device(): netted = jnp.dot(arrived, onehot, preferred_element_type=jnp.float32)  14 us
    gather x2, local copies, waits for them, and re-layouts, on_device(): jnp.take(described, chosen, axis=1)  12.8 us
    all_to_all x1, starting transfers between devices, on_device(): lax.all_to_all(labels, 'cpty', split_axis=1, concat_axis=1, tiled=True)  11.5 us
    all_to_all x1, starting transfers between devices, on_device(): lax.all_to_all(packed, 'cpty', split_axis=1, concat_axis=1, tiled=True)  9.77 us
  transfers between devices with their start and end apart: 3, of which 2 were waited for; matrix products, arithmetic and copies ran while one was open for 6% of the time, Pallas kernels for 0%

commit v1 on v0

v1 whole, which is shorter than its diff:
```python
import jax
import jax.numpy as jnp
from jax import lax
from jax.experimental import pallas as pl
from jax.experimental.pallas import tpu as pltpu
from jax.sharding import PartitionSpec as P

NP, NZ, NY = 8, 8, 4
CP = 128
ROWS = 80
SLOT = 128
F = 64
CH = 4
BF, F32 = jnp.bfloat16, jnp.float32
NT = (((1,), (1,)), ((), ()))


def remote(src, dst, ssem, rsem, p, c):
    return pltpu.make_async_remote_copy(
        src_ref=src, dst_ref=dst, send_sem=ssem, recv_sem=rsem,
        device_id={"paths": p, "cpty": c}, device_id_type=pl.DeviceIdType.MESH,
    )


def kernel(fac_ref, load_ref, term_ref, id_ref, exp_ref, mom_ref,
           desc, pack, trades, hot, ft, net, own, at, rm, rp, acc, rsb, rr, fs, fr,
           s1, r1, s2, r2, sy, ry, szp, rzp, szm, rzm, srs, rrs, sf, rf):
    p = lax.axis_index("paths")
    c = lax.axis_index("cpty")
    z, y = c // NY, c % NY
    paths = fac_ref.shape[1]
    rows = paths // CH
    count = id_ref.shape[1]
    first = lax.rem(p - c + 32, 8)
    targets = [first + 8 * i for i in range(4)]
    up, down = lax.rem(z + 1, NZ) * NY + y, lax.rem(z + NZ - 1, NZ) * NY + y

    barrier = pltpu.get_barrier_semaphore()

    def greet(pp, cc):
        pl.semaphore_signal(barrier, inc=1, device_id={"paths": pp, "cpty": cc},
                            device_id_type=pl.DeviceIdType.MESH)

    for k in targets:
        @pl.when(k != c)
        def _(k=k):
            greet(p, k)
    for r in range(1, NP):
        greet(lax.rem(p + r, NP), c)
    greet(p, up)
    greet(p, down)
    for r in range(1, NY):
        greet(p, z * NY + lax.rem(y + r, NY))

    desc[0:F, :] = load_ref[...]
    desc[F:ROWS, :] = term_ref[...]
    ids = id_ref[...]
    owner = ids // CP
    block = 256
    upper = (lax.broadcasted_iota(jnp.int32, (block, block), 0)
             < lax.broadcasted_iota(jnp.int32, (block, block), 1)).astype(BF)
    eq = (lax.broadcasted_iota(jnp.int32, (NZ * NY, count), 0) == owner).astype(F32)
    base = jnp.zeros((NZ * NY, 1), F32)
    ranks = []
    for b in range(count // block):
        part = eq[:, b * block:(b + 1) * block]
        before = jnp.dot(part.astype(BF), upper, preferred_element_type=F32) + base
        base = base + jnp.sum(part, axis=1, keepdims=True)
        ranks.append(jnp.sum(part * before, axis=0, keepdims=True))
    rank = jnp.concatenate(ranks, axis=1).astype(jnp.int32)
    mine = lax.rem(owner + c, 8) == p
    code = jnp.where(mine, (owner // 8) * SLOT + rank, -1)
    total = jnp.zeros((ROWS, 4 * SLOT), F32)
    step = 512
    for b in range(count // step):
        cols = slice(b * step, (b + 1) * step)
        chosen = (lax.broadcasted_iota(jnp.int32, (4 * SLOT, step), 0) == code[:, cols]).astype(F32).astype(BF)
        total = total + lax.dot_general(desc[:, cols], chosen, NT, preferred_element_type=F32)
    for i in range(4):
        pack[i] = total[:, i * SLOT:(i + 1) * SLOT].astype(BF)
    ft[...] = jnp.transpose(fac_ref[...].astype(F32)).astype(BF)

    pl.semaphore_wait(barrier, NP - 1 + 2 + NY - 1 + 4 - (lax.rem(2 * c, 8) == p).astype(jnp.int32))

    place = c // 8
    for i, k in enumerate(targets):
        copy = remote(pack.at[i], trades.at[p, place], s1.at[i], r1.at[place], p, k)

        @pl.when(k != c)
        def _(copy=copy):
            copy.start()

        @pl.when(k == c)
        def _(i=i):
            trades[p, place] = pack[i]
    for i, k in enumerate(targets):
        arrive = remote(pack.at[i], trades.at[p, i], s1.at[i], r1.at[i], p, k)

        @pl.when(k != c)
        def _(arrive=arrive):
            arrive.wait_recv()
    spread = []
    for r in range(1, NP):
        copy = remote(trades.at[p], trades.at[p], s2.at[r], r2.at[r], lax.rem(p + r, NP), c)
        copy.start()
        spread.append(copy)

    def tile_of(pp):
        t = trades[pp]
        return jnp.concatenate([t[i] for i in range(4)], axis=1)

    def price(j, pp):
        full = tile_of(pp)
        terms = full[F:ROWS, :].astype(F32)
        lin = jnp.dot(ft[j * rows:(j + 1) * rows, :], full[0:F, :], preferred_element_type=F32)
        value = terms[0:1, :] * (lin + terms[2:3, :] * jnp.tanh(lin - terms[1:2, :]))
        return lax.dot_general(value.astype(BF), hot[pp], NT, preferred_element_type=F32)

    sends = []

    def go(copy):
        copy.start()
        sends.append(copy)

    def ring(s, j):
        pair = []
        if s < 3 or j < 2:
            src = own.at[j] if s == 0 else rm.at[s - 1, j]
            pair.append(remote(src, rm.at[s, j], szp.at[s, j], rzp.at[s, j], p, up))
        if s < 3 or j >= 2:
            src = own.at[j] if s == 0 else rp.at[s - 1, j]
            pair.append(remote(src, rp.at[s, j], szm.at[s, j], rzm.at[s, j], p, down))
        return pair

    def add(slot, j, value):
        if j == 0:
            acc[slot] = value
        else:
            acc[slot] += value

    def left(j):
        return at[j].reshape(NY * CP, rows)

    def ship(d):
        rsb[d] = acc[d].astype(BF)
        zz = lax.rem(z + d, NZ)
        r = lax.rem(zz - p + NP, NP)
        copy = remote(rsb.at[d], rr.at[r], srs.at[d], rrs.at[r], zz, c)

        @pl.when(r != 0)
        def _():
            copy.start()

    for t in range(CH + 4):
        if t < CH:
            j = t
            net[...] = jnp.zeros_like(net)

            def body(r, _):
                pp = lax.rem(p + r, NP)
                if j == 0:
                    @pl.when(r > 0)
                    def _():
                        src = lax.rem(p - r + NP, NP)
                        remote(trades.at[src], trades.at[src], s2.at[r], r2.at[r], src, c).wait_recv()

                    pp = lax.rem(p - r + NP, NP)
                    t4 = trades[pp]
                    label = jnp.concatenate([t4[i][F:ROWS, :] for i in range(4)], axis=1).astype(F32)[3:4, :]
                    hot[pp] = (lax.broadcasted_iota(jnp.int32, (CP, 4 * SLOT), 0).astype(F32) == label).astype(F32).astype(BF)
                net[...] += price(j, pp)
                return 0

            lax.fori_loop(0, NP, body, 0)
            block_f = jnp.maximum(net[...], 0.0)
            block_b = block_f.astype(BF)
            own[j] = block_b
            exp_ref[j * rows:(j + 1) * rows, :] = block_b
            at[j, y] = jnp.transpose(block_f).astype(BF)
            for copy in ring(0, j):
                go(copy)
            for r in range(1, NY):
                go(remote(at.at[j, y], at.at[j, y], sy.at[j, r], ry.at[j, r], p, z * NY + lax.rem(y + r, NY)))
        for s in (1, 2, 3):
            j = t - s
            if 0 <= j < CH:
                for copy in ring(s - 1, j):
                    copy.wait_recv()
                for copy in ring(s, j):
                    go(copy)
        j = t - 1
        if 0 <= j < CH:
            for r in range(1, NY):
                src = lax.rem(y + NY - r, NY)
                remote(at.at[j, src], at.at[j, src], sy.at[j, r], ry.at[j, r], p, z * NY + src).wait_recv()
            add(0, j, jnp.dot(left(j), own[j], preferred_element_type=F32))
        for s in (1, 2, 3):
            j = t - s
            if 0 <= j < CH:
                both = jnp.concatenate([rm[s - 1, j], rp[s - 1, j]], axis=1)
                res = jnp.dot(left(j), both, preferred_element_type=F32)
                add(NZ - s, j, res[:, :CP])
                add(s, j, res[:, CP:])
        j = t - 4
        if 0 <= j < CH:
            for copy in ring(3, j):
                copy.wait_recv()
            far = rm[3, j] if j < 2 else rp[3, j]
            add(4, j, jnp.dot(left(j), far, preferred_element_type=F32))
        if t >= 4:
            done = {4: (0, 1, 7), 5: (2, 6), 6: (3, 5), 7: (4,)}[t]
            for d in done:
                ship(d)

    whole = rsb[lax.rem(p - z + NP, NP)].astype(F32)
    for r in range(1, NP):
        src = lax.rem(p - r + NP, NP)
        remote(rsb.at[0], rr.at[r], srs.at[0], rrs.at[r], src, c).wait_recv()
        whole = whole + rr[r].astype(F32)
    whole = whole * (1.0 / (paths * NP))
    for i in range(NY):
        fs[i] = jnp.transpose(whole[i * CP:(i + 1) * CP, :]).astype(BF)
    for r in range(1, NY):
        yy = lax.rem(y + r, NY)
        go(remote(fs.at[yy], fr.at[r], sf.at[r], rf.at[r], p, z * NY + yy))
    mom_ref[y] = fs[y].astype(F32)
    for r in range(1, NY):
        src = lax.rem(y + NY - r, NY)
        remote(fs.at[src], fr.at[r], sf.at[r], rf.at[r], p, z * NY + src).wait_recv()
        mom_ref[src] = fr[r].astype(F32)

    for i, k in enumerate(targets):
        copy = remote(pack.at[i], trades.at[p, place], s1.at[i], r1.at[place], p, k)

        @pl.when(k != c)
        def _(copy=copy):
            copy.wait_send()
    for copy in spread:
        copy.wait_send()
    for copy in sends:
        copy.wait_send()
    for d in range(NZ):
        zz = lax.rem(z + d, NZ)
        r = lax.rem(zz - p + NP, NP)
        copy = remote(rsb.at[d], rr.at[r], srs.at[d], rrs.at[r], zz, c)

        @pl.when(r != 0)
        def _(copy=copy):
            copy.wait_send()


def on_device(factors, loadings, notional, strike, curvature, trade_cpty):
    count, paths = loadings.shape[1], factors.shape[1]
    rows = paths // CH
    local = (trade_cpty % CP).astype(BF)
    terms = jnp.concatenate(
        [jnp.stack([notional, strike, curvature, local]), jnp.zeros((ROWS - F - 4, count), BF)], axis=0)
    vmem = pl.BlockSpec(memory_space=pltpu.VMEM)
    dma = pltpu.SemaphoreType.DMA
    exposure, moment = pl.pallas_call(
        kernel,
        out_shape=(jax.ShapeDtypeStruct((paths, CP), BF), jax.ShapeDtypeStruct((NY, CP, CP), F32)),
        in_specs=[vmem] * 4,
        out_specs=(vmem, vmem),
        scratch_shapes=[
            pltpu.VMEM((ROWS, count), BF),
            pltpu.VMEM((4, ROWS, SLOT), BF),
            pltpu.VMEM((NP, 4, ROWS, SLOT), BF),
            pltpu.VMEM((NP, CP, 4 * SLOT), BF),
            pltpu.VMEM((paths, F), BF),
            pltpu.VMEM((rows, CP), F32),
            pltpu.VMEM((CH, rows, CP), BF),
            pltpu.VMEM((CH, NY, CP, rows), BF),
            pltpu.VMEM((4, CH, rows, CP), BF),
            pltpu.VMEM((4, CH, rows, CP), BF),
            pltpu.VMEM((NZ, NY * CP, CP), F32),
            pltpu.VMEM((NZ, NY * CP, CP), BF),
            pltpu.VMEM((NP, NY * CP, CP), BF),
            pltpu.VMEM((NY, CP, CP), BF),
            pltpu.VMEM((NY, CP, CP), BF),
            dma((4,)), dma((4,)), dma((NP,)), dma((NP,)),
            dma((CH, NY)), dma((CH, NY)),
            dma((4, CH)), dma((4, CH)), dma((4, CH)), dma((4, CH)),
            dma((NZ,)), dma((NP,)), dma((NY,)), dma((NY,)),
        ],
        compiler_params=pltpu.CompilerParams(
            collective_id=0, has_side_effects=True, vmem_limit_bytes=50 * 1024 * 1024),
    )(factors, loadings, terms, trade_cpty[None, :])
    return exposure, moment.reshape(NY * CP, CP)


def solution(mesh):
    in_specs = (P(None, "paths"), P(None, "cpty"), P("cpty"), P("cpty"), P("cpty"), P("cpty"))
    out_specs = (P("paths", "cpty"), P("paths", "cpty"))
    return jax.shard_map(
        on_device, mesh=mesh, in_specs=in_specs, out_specs=out_specs, check_vma=False
    )
```

time: 288 us -> 85.7 us (0.30); the launches traced: 284 us -> 85.4 us
  waiting for transfers between devices: 139 us -> 0 us
  Pallas kernels: 0 us -> 78.8 us
  local copies, waits for them, and re-layouts: 54.7 us -> 5.15 us
  matrix products: 22.1 us -> 0 us
  starting transfers between devices: 21.3 us -> 0 us
  blocking collectives: 17.5 us -> 0 us
  other arithmetic: 15 us -> 0.75 us
  between operations: 14.3 us -> 0.68 us
    all_gather x1 -> x0, waiting for transfers between devices: 122 us -> none  [on_device(): everyone = lax.all_gather(exposure, 'cpty', axis=1, tiled=True)]
    pallas_call x0 -> x1, Pallas kernels: none -> 78.8 us  [on_device(): pl.pallas_call(kernel, out_shape=(jax.ShapeDtypeStruct((paths, CP), BF),...]
    gather x3 -> x0, local copies, waits for them, and re-layouts: 35.8 us -> none  [the longest x1 23 us: on_device(): labels = jnp.where(filled, trade_cpty[chosen], -1)[None, :]]
    dot_general x2 -> x0, matrix products: 22.1 us -> none  [the longest x1 14 us: on_device(): netted = jnp.dot(arrived, onehot, preferred_element_type=jnp.float32)]
    all_to_all x2 -> x0, starting transfers between devices: 21.3 us -> none  [the longest x1 11.5 us: on_device(): lax.all_to_all(labels, 'cpty', split_axis=1, concat_axis=1, tiled=True)]
    all_to_all x1 -> x0, blocking collectives: 17.5 us -> none  [summed_on_arrival(): lax.all_to_all(parts, axis, split_axis=0, concat_axis=0, tiled=True)]
    all_to_all x2 -> x0, waiting for transfers between devices: 17.5 us -> none  [the longest x1 17.5 us: on_device(): lax.all_to_all(packed, 'cpty', split_axis=1, concat_axis=1, tiled=True)]
    scatter x2 -> x0, local copies, waits for them, and re-layouts: 17.2 us -> none  [the longest x1 9.13 us: on_device(): filled = jnp.zeros((groups * slot_size,), jnp.bool_).at[target].set(True)]
  transfers between devices with their start and end apart: 3 -> 0, of which waited for: 2 -> 0; matrix products, arithmetic and copies ran while one was open for 6% -> 0% of each run, Pallas kernels for 0% -> 0%
where the time goes in v1:
time: 85.7 us; the launch traced here: 85.4 us
  Pallas kernels  78.8 us (92%)
  local copies, waits for them, and re-layouts  5.15 us (6%)
    pallas_call x1, Pallas kernels, on_device(): pl.pallas_call(kernel, out_shape=(jax.ShapeDtypeStruct((paths, CP), BF),...  78.8 us
    unnamed x8, local copies, waits for them, and re-layouts  2.81 us
    another operation x4, local copies, waits for them, and re-layouts, on_device(): jnp.stack([notional, strike, curvature, local])  2.09 us

profile of v1, /device:TPU:4, one launch (start us, length us, event | category | flops | bytes accessed | tf_op | source)
XLA Modules:
  0.0 85.4 jit_solution(9006521878932819744)
XLA Ops:
  0.6 0.0 copy-start
  0.6 0.8 fusion.1
  1.4 0.7 stack.12
  2.1 0.7 stack.13
  2.8 0.7 stack.14
  3.5 0.0 copy-start.2
  3.5 0.2 concatenate.3.term_ref
  3.8 0.0 copy-done
  3.8 0.4 copy-done.2
  4.2 0.0 copy-start.1
  4.2 0.9 %copy-done.1 = bf16[64,1536]{1,0:T(8,128)(2,1)S(1)} copy-done((bf16[64,1536]{1,0:T(8,128)(2,1)S(1)}, bf16[64,1536]{1,0:T(8,128)(2,1)}, u32[]{:S(2)}) %copy-start.1) | copy-done | bytes 196632
  5.1 78.8 %shard_map.77 = (bf16[1536,128]{1,0:T(8,128)(2,1)S(1)}, f32[4,128,128]{2,1,0:T(8,128)S(1)}) custom-call(bf16[64,1536]{1,0:T(8,128)(2,1)S(1)} %copy-done.1, bf16[64,2048]{1,0:T(8,128)(2,1)S(1)} %copy-done, bf16[16,2048]{1,0:T(8,128)(2,1)S(1)} %concatenate.3.term_ref, s32[1,2048]{1,0:T(1,128)S(1)} %bitcast.3), custom_call_target="tpu_custom_call" | custom-call | tf_op jit(solution)/shard_map/pallas_call | solution.py:260
  83.9 0.7 copy.10
  84.7 0.7 copy.11
  (2 shorter events, 0.0 us)
Async XLA Ops:
  0.6 3.1 %copy-start = (bf16[64,2048]{1,0:T(8,128)(2,1)S(1)}, bf16[64,2048]{1,0:T(8,128)(2,1)}, u32[]{:S(2)}) copy-start(bf16[64,2048]{1,0:T(8,128)(2,1)} %load_ref.1) | copy-start | bytes 786436
  3.5 0.7 copy-start.2
  4.2 0.9 %copy-start.1 = (bf16[64,1536]{1,0:T(8,128)(2,1)S(1)}, bf16[64,1536]{1,0:T(8,128)(2,1)}, u32[]{:S(2)}) copy-start(bf16[64,1536]{1,0:T(8,128)(2,1)} %fac_ref.1) | copy-start | bytes 589828

commit v2 on v1

--- a/solution.py
+++ b/solution.py
@@ -5,7 +5,8 @@
 from jax.experimental.pallas import tpu as pltpu
 from jax.sharding import PartitionSpec as P
 
-NP, NZ, NY = 8, 8, 4
+NP, NX, NZ, NY = 8, 4, 8, 4
+FAR = 4
 CP = 128
 ROWS = 80
 SLOT = 128
@@ -23,8 +24,8 @@
 
 
 def kernel(fac_ref, load_ref, term_ref, id_ref, exp_ref, mom_ref,
-           desc, pack, trades, hot, ft, net, own, at, rm, rp, acc, rsb, rr, fs, fr,
-           s1, r1, s2, r2, sy, ry, szp, rzp, szm, rzm, srs, rrs, sf, rf):
+           desc, pack, trades, hot, ft, net, own, at, ring_in, acc, rsb, rr, keep, turn, fa, fb,
+           s1, r1, s2, r2, sy, ry, sz, rz, srs, rrs, sa, ra, sb, rb):
     p = lax.axis_index("paths")
     c = lax.axis_index("cpty")
     z, y = c // NY, c % NY
@@ -33,7 +34,11 @@
     count = id_ref.shape[1]
     first = lax.rem(p - c + 32, 8)
     targets = [first + 8 * i for i in range(4)]
-    up, down = lax.rem(z + 1, NZ) * NY + y, lax.rem(z + NZ - 1, NZ) * NY + y
+    x, core = p // 2, p % 2
+    sign = 1 - 2 * core
+    ahead, behind = lax.rem(z - sign + NZ, NZ), lax.rem(z + sign + NZ, NZ)
+    y_ahead, y_back = lax.rem(y - sign + NY, NY), lax.rem(y + sign + NY, NY)
+    far_here, far_ahead = z // FAR, ahead // FAR
 
     barrier = pltpu.get_barrier_semaphore()
 
@@ -47,8 +52,8 @@
             greet(p, k)
     for r in range(1, NP):
         greet(lax.rem(p + r, NP), c)
-    greet(p, up)
-    greet(p, down)
+    greet(p, ahead * NY + y)
+    greet(p, behind * NY + y)
     for r in range(1, NY):
         greet(p, z * NY + lax.rem(y + r, NY))
 
@@ -123,35 +128,67 @@
         sends.append(copy)
 
     def ring(s, j):
-        pair = []
-        if s < 3 or j < 2:
-            src = own.at[j] if s == 0 else rm.at[s - 1, j]
-            pair.append(remote(src, rm.at[s, j], szp.at[s, j], rzp.at[s, j], p, up))
-        if s < 3 or j >= 2:
-            src = own.at[j] if s == 0 else rp.at[s - 1, j]
-            pair.append(remote(src, rp.at[s, j], szm.at[s, j], rzm.at[s, j], p, down))
-        return pair
-
-    def add(slot, j, value):
-        if j == 0:
-            acc[slot] = value
+        src = own.at[j] if s == 0 else ring_in.at[s - 1, j]
+        slot = j if s < FAR - 1 else j // 2
+        return remote(src, ring_in.at[s, slot], sz.at[s, slot], rz.at[s, slot], p, ahead * NY + y)
+
+    def side(j, way):
+        origin = y if way < 2 else y_back
+        target = y_back if way == 1 else y_ahead
+        return remote(at.at[j, origin], at.at[j, origin], sy.at[j, way], ry.at[j, way], p, z * NY + target)
+
+    def side_wait(j, way):
+        origin = (y_back, y_ahead, lax.rem(y + 2, NY))[way]
+        remote(at.at[j, origin], at.at[j, origin], sy.at[j, way], ry.at[j, way], p, z * NY + y_back).wait_recv()
+
+    def add(d, j, value, start):
+        if start:
+            acc[d] = value
         else:
-            acc[slot] += value
+            acc[d] += value
 
     def left(j):
         return at[j].reshape(NY * CP, rows)
 
+    def cell(d):
+        return lax.rem(z + sign * d + NZ, NZ)
+
     def ship(d):
-        rsb[d] = acc[d].astype(BF)
-        zz = lax.rem(z + d, NZ)
-        r = lax.rem(zz - p + NP, NP)
-        copy = remote(rsb.at[d], rr.at[r], srs.at[d], rrs.at[r], zz, c)
-
-        @pl.when(r != 0)
+        rsb[d] = acc[d].reshape(NY, CP, CP).astype(BF)
+        for r in range(1, NX):
+            xx = lax.rem(x + r, NX)
+            go(remote(rsb.at[d, xx], rr.at[d, r], srs.at[d, r], rrs.at[d, r], 2 * xx + core, c))
+
+    def turned(d):
+        return remote(turn.at[d], fa.at[core, y], sa.at[d], ra.at[core, y], cell(d), z * NY + x)
+
+    def turned_home(d):
+        return (cell(d) == p) & (x == y)
+
+    def direct(d):
+        return remote(keep.at[d], fb.at[core, x], sb.at[d], rb.at[core, x], z, cell(d) * NY + y)
+
+    def collect(d):
+        whole = acc[d, pl.ds(pl.multiple_of(x * CP, CP), CP), :]
+        for r in range(1, NX):
+            src = lax.rem(x - r + NX, NX)
+            remote(rsb.at[d, src], rr.at[d, r], srs.at[d, r], rrs.at[d, r], 2 * src + core, c).wait_recv()
+            whole = whole + rr[d, r].astype(F32)
+        whole = whole * (1.0 / (paths * NP))
+        if d > 0:
+            keep[d] = whole.astype(BF)
+            go(direct(d))
+        turn[d] = jnp.transpose(whole).astype(BF)
+
+        @pl.when(jnp.logical_not(turned_home(d)))
         def _():
-            copy.start()
-
-    for t in range(CH + 4):
+            turned(d).start()
+
+        @pl.when(turned_home(d))
+        def _():
+            fa[core, y] = turn[d]
+
+    for t in range(CH + FAR):
         if t < CH:
             j = t
             net[...] = jnp.zeros_like(net)
@@ -177,57 +214,70 @@
             own[j] = block_b
             exp_ref[j * rows:(j + 1) * rows, :] = block_b
             at[j, y] = jnp.transpose(block_f).astype(BF)
-            for copy in ring(0, j):
-                go(copy)
-            for r in range(1, NY):
-                go(remote(at.at[j, y], at.at[j, y], sy.at[j, r], ry.at[j, r], p, z * NY + lax.rem(y + r, NY)))
-        for s in (1, 2, 3):
+            go(ring(0, j))
+            go(side(j, 0))
+            go(side(j, 1))
+        for s in range(1, FAR):
             j = t - s
             if 0 <= j < CH:
-                for copy in ring(s - 1, j):
-                    copy.wait_recv()
-                for copy in ring(s, j):
-                    go(copy)
+                ring(s - 1, j).wait_recv()
+                if s < FAR - 1:
+                    go(ring(s, j))
+                else:
+                    copy = ring(s, j)
+
+                    @pl.when(far_ahead == j % 2)
+                    def _(copy=copy):
+                        copy.start()
         j = t - 1
         if 0 <= j < CH:
-            for r in range(1, NY):
-                src = lax.rem(y + NY - r, NY)
-                remote(at.at[j, src], at.at[j, src], sy.at[j, r], ry.at[j, r], p, z * NY + src).wait_recv()
-            add(0, j, jnp.dot(left(j), own[j], preferred_element_type=F32))
-        for s in (1, 2, 3):
-            j = t - s
-            if 0 <= j < CH:
-                both = jnp.concatenate([rm[s - 1, j], rp[s - 1, j]], axis=1)
-                res = jnp.dot(left(j), both, preferred_element_type=F32)
-                add(NZ - s, j, res[:, :CP])
-                add(s, j, res[:, CP:])
-        j = t - 4
+            side_wait(j, 0)
+            go(side(j, 2))
+            side_wait(j, 1)
+        j = t - 2
         if 0 <= j < CH:
-            for copy in ring(3, j):
-                copy.wait_recv()
-            far = rm[3, j] if j < 2 else rp[3, j]
-            add(4, j, jnp.dot(left(j), far, preferred_element_type=F32))
-        if t >= 4:
-            done = {4: (0, 1, 7), 5: (2, 6), 6: (3, 5), 7: (4,)}[t]
-            for d in done:
+            side_wait(j, 2)
+            add(0, j, jnp.dot(left(j), own[j], preferred_element_type=F32), j == 0)
+            add(1, j, jnp.dot(left(j), ring_in[0, j], preferred_element_type=F32), j == 0)
+            add(2, j, jnp.dot(left(j), ring_in[1, j], preferred_element_type=F32), j == 0)
+        j = t - 3
+        if 0 <= j < CH:
+            add(3, j, jnp.dot(left(j), ring_in[2, j], preferred_element_type=F32), j == 0)
+        j = t - FAR
+        if 0 <= j < CH:
+            @pl.when(far_here == j % 2)
+            def _(j=j):
+                ring(FAR - 1, j).wait_recv()
+                add(FAR, j, jnp.dot(left(j), ring_in[FAR - 1, j // 2], preferred_element_type=F32), j < 2)
+        if t == 5:
+            for d in (0, 1, 2):
                 ship(d)
-
-    whole = rsb[lax.rem(p - z + NP, NP)].astype(F32)
-    for r in range(1, NP):
-        src = lax.rem(p - r + NP, NP)
-        remote(rsb.at[0], rr.at[r], srs.at[0], rrs.at[r], src, c).wait_recv()
-        whole = whole + rr[r].astype(F32)
-    whole = whole * (1.0 / (paths * NP))
-    for i in range(NY):
-        fs[i] = jnp.transpose(whole[i * CP:(i + 1) * CP, :]).astype(BF)
-    for r in range(1, NY):
-        yy = lax.rem(y + r, NY)
-        go(remote(fs.at[yy], fr.at[r], sf.at[r], rf.at[r], p, z * NY + yy))
-    mom_ref[y] = fs[y].astype(F32)
-    for r in range(1, NY):
-        src = lax.rem(y + NY - r, NY)
-        remote(fs.at[src], fr.at[r], sf.at[r], rf.at[r], p, z * NY + src).wait_recv()
-        mom_ref[src] = fr[r].astype(F32)
+        if t == 6:
+            ship(3)
+            for d in (0, 1, 2):
+                collect(d)
+    ship(FAR)
+    collect(3)
+    collect(FAR)
+
+    delta = lax.rem(p - z + NZ, NZ)
+    mom_ref[...] = jnp.zeros_like(mom_ref)
+    for k in range(2):
+        near = (delta <= FAR) if k == 0 else ((delta >= FAR) | (delta == 0))
+        away = ((delta >= FAR) if k == 0 else ((delta <= FAR) & (delta > 0)))
+        for i in range(NY):
+            @pl.when(near & jnp.logical_not((core == k) & (i == y) & (x == y)))
+            def _(k=k, i=i):
+                remote(turn.at[0], fa.at[k, i], sa.at[0], ra.at[k, i], 2 * y + k, z * NY + i).wait_recv()
+
+            @pl.when(near)
+            def _(k=k, i=i):
+                mom_ref[i] += fa[k, i].astype(F32)
+
+            @pl.when(away)
+            def _(k=k, i=i):
+                remote(turn.at[0], fb.at[k, i], sb.at[0], rb.at[k, i], 2 * i + k, p * NY + y).wait_recv()
+                mom_ref[i] += fb[k, i].astype(F32)
 
     for i, k in enumerate(targets):
         copy = remote(pack.at[i], trades.at[p, place], s1.at[i], r1.at[place], p, k)
@@ -239,14 +289,16 @@
         copy.wait_send()
     for copy in sends:
         copy.wait_send()
-    for d in range(NZ):
-        zz = lax.rem(z + d, NZ)
-        r = lax.rem(zz - p + NP, NP)
-        copy = remote(rsb.at[d], rr.at[r], srs.at[d], rrs.at[r], zz, c)
-
-        @pl.when(r != 0)
+    for j in range(CH):
+        copy = ring(FAR - 1, j)
+
+        @pl.when(far_ahead == j % 2)
         def _(copy=copy):
             copy.wait_send()
+    for d in range(FAR + 1):
+        @pl.when(jnp.logical_not(turned_home(d)))
+        def _(d=d):
+            turned(d).wait_send()
 
 
 def on_device(factors, loadings, notional, strike, curvature, trade_cpty):
@@ -271,17 +323,18 @@
             pltpu.VMEM((rows, CP), F32),
             pltpu.VMEM((CH, rows, CP), BF),
             pltpu.VMEM((CH, NY, CP, rows), BF),
-            pltpu.VMEM((4, CH, rows, CP), BF),
-            pltpu.VMEM((4, CH, rows, CP), BF),
-            pltpu.VMEM((NZ, NY * CP, CP), F32),
-            pltpu.VMEM((NZ, NY * CP, CP), BF),
-            pltpu.VMEM((NP, NY * CP, CP), BF),
-            pltpu.VMEM((NY, CP, CP), BF),
-            pltpu.VMEM((NY, CP, CP), BF),
+            pltpu.VMEM((FAR, CH, rows, CP), BF),
+            pltpu.VMEM((FAR + 1, NY * CP, CP), F32),
+            pltpu.VMEM((FAR + 1, NY, CP, CP), BF),
+            pltpu.VMEM((FAR + 1, NX, CP, CP), BF),
+            pltpu.VMEM((FAR + 1, CP, CP), BF),
+            pltpu.VMEM((FAR + 1, CP, CP), BF),
+            pltpu.VMEM((2, NY, CP, CP), BF),
+            pltpu.VMEM((2, NX, CP, CP), BF),
             dma((4,)), dma((4,)), dma((NP,)), dma((NP,)),
-            dma((CH, NY)), dma((CH, NY)),
-            dma((4, CH)), dma((4, CH)), dma((4, CH)), dma((4, CH)),
-            dma((NZ,)), dma((NP,)), dma((NY,)), dma((NY,)),
+            dma((CH, 3)), dma((CH, 3)), dma((FAR, CH)), dma((FAR, CH)),
+            dma((FAR + 1, NX)), dma((FAR + 1, NX)),
+            dma((FAR + 1,)), dma((2, NY)), dma((FAR + 1,)), dma((2, NX)),
         ],
         compiler_params=pltpu.CompilerParams(
             collective_id=0, has_side_effects=True, vmem_limit_bytes=50 * 1024 * 1024),

time: 85.7 us -> 74 us (0.86)
  Pallas kernels: 78.8 us -> 67.1 us
    pallas_call x1, Pallas kernels: 78.8 us -> 67.1 us  [on_device(): pl.pallas_call(kernel, out_shape=(jax.ShapeDtypeStruct((paths, CP), BF),...]
where the time goes in v2:
time: 74 us; the launch traced here: 73.7 us
  Pallas kernels  67.1 us (91%)
  local copies, waits for them, and re-layouts  5.15 us (7%)
  other arithmetic  0.75 us (1%)
    pallas_call x1, Pallas kernels, on_device(): pl.pallas_call(kernel, out_shape=(jax.ShapeDtypeStruct((paths, CP), BF),...  67.1 us
    unnamed x8, local copies, waits for them, and re-layouts  2.81 us
    another operation x4, local copies, waits for them, and re-layouts, on_device(): jnp.stack([notional, strike, curvature, local])  2.09 us

profile of v2, /device:TPU:4, one launch (start us, length us, event | category | flops | bytes accessed | tf_op | source)
XLA Modules:
  0.0 73.7 jit_solution(10833683496198265326)
XLA Ops:
  0.6 0.0 copy-start
  0.6 0.8 %fusion.1 = bf16[2048]{0:T(1024)(128)(2,1)S(1)} fusion(s32[2048]{0:T(1024)} %param.11), kind=kLoop, calls=%fused_computation.4 | loop fusion | flops 24576 | bytes 12288 | tf_op jit(solution)/shard_map/convert_element_type | solution.py:307
  1.4 0.7 stack.12
  2.1 0.7 stack.13
  2.8 0.7 stack.14
  3.5 0.0 copy-start.2
  3.5 0.2 concatenate.3.term_ref
  3.8 0.0 copy-done
  3.8 0.4 copy-done.2
  4.2 0.0 copy-start.1
  4.2 0.9 %copy-done.1 = bf16[64,1536]{1,0:T(8,128)(2,1)S(1)} copy-done((bf16[64,1536]{1,0:T(8,128)(2,1)S(1)}, bf16[64,1536]{1,0:T(8,128)(2,1)}, u32[]{:S(2)}) %copy-start.1) | copy-done | bytes 196632
  5.1 67.1 %shard_map.77 = (bf16[1536,128]{1,0:T(8,128)(2,1)S(1)}, f32[4,128,128]{2,1,0:T(8,128)S(1)}) custom-call(bf16[64,1536]{1,0:T(8,128)(2,1)S(1)} %copy-done.1, bf16[64,2048]{1,0:T(8,128)(2,1)S(1)} %copy-done, bf16[16,2048]{1,0:T(8,128)(2,1)S(1)} %concatenate.3.term_ref, s32[1,2048]{1,0:T(1,128)S(1)} %bitcast.3), custom_call_target="tpu_custom_call" | custom-call | tf_op jit(solution)/shard_map/pallas_call | solution.py:312
  72.2 0.7 %copy.10 = bf16[1536,128]{1,0:T(8,128)(2,1)} copy(bf16[1536,128]{1,0:T(8,128)(2,1)S(1)} %get-tuple-element.8) | data formatting | bytes 786432
  73.0 0.7 copy.11
  (2 shorter events, 0.0 us)
Async XLA Ops:
  0.6 3.1 %copy-start = (bf16[64,2048]{1,0:T(8,128)(2,1)S(1)}, bf16[64,2048]{1,0:T(8,128)(2,1)}, u32[]{:S(2)}) copy-start(bf16[64,2048]{1,0:T(8,128)(2,1)} %load_ref.1) | copy-start | bytes 786436
  3.5 0.7 copy-start.2
  4.2 0.9 %copy-start.1 = (bf16[64,1536]{1,0:T(8,128)(2,1)S(1)}, bf16[64,1536]{1,0:T(8,128)(2,1)}, u32[]{:S(2)}) copy-start(bf16[64,1536]{1,0:T(8,128)(2,1)} %fac_ref.1) | copy-start | bytes 589828

commit v3 on v2

--- a/solution.py
+++ b/solution.py
@@ -188,7 +188,7 @@
         def _():
             fa[core, y] = turn[d]
 
-    for t in range(CH + FAR):
+    for t in range(CH + FAR + 1):
         if t < CH:
             j = t
             net[...] = jnp.zeros_like(net)
@@ -208,7 +208,7 @@
                 net[...] += price(j, pp)
                 return 0
 
-            lax.fori_loop(0, NP, body, 0)
+            lax.fori_loop(0, NP, body, 0, unroll=1 if j == 0 else NP)
             block_f = jnp.maximum(net[...], 0.0)
             block_b = block_f.astype(BF)
             own[j] = block_b
@@ -218,7 +218,7 @@
             go(side(j, 0))
             go(side(j, 1))
         for s in range(1, FAR):
-            j = t - s
+            j = t - 1 - s
             if 0 <= j < CH:
                 ring(s - 1, j).wait_recv()
                 if s < FAR - 1:
@@ -229,36 +229,34 @@
                     @pl.when(far_ahead == j % 2)
                     def _(copy=copy):
                         copy.start()
-        j = t - 1
+        j = t - 2
         if 0 <= j < CH:
             side_wait(j, 0)
             go(side(j, 2))
             side_wait(j, 1)
-        j = t - 2
+        j = t - 3
         if 0 <= j < CH:
             side_wait(j, 2)
             add(0, j, jnp.dot(left(j), own[j], preferred_element_type=F32), j == 0)
-            add(1, j, jnp.dot(left(j), ring_in[0, j], preferred_element_type=F32), j == 0)
-            add(2, j, jnp.dot(left(j), ring_in[1, j], preferred_element_type=F32), j == 0)
-        j = t - 3
+            for d in (1, 2):
+                add(d, j, jnp.dot(left(j), ring_in[d - 1, j], preferred_element_type=F32), j == 0)
+            if j == CH - 1:
+                for d in (0, 1, 2):
+                    ship(d)
+        j = t - 4
         if 0 <= j < CH:
             add(3, j, jnp.dot(left(j), ring_in[2, j], preferred_element_type=F32), j == 0)
-        j = t - FAR
+            if j == CH - 1:
+                ship(3)
+        j = t - 1 - FAR
         if 0 <= j < CH:
             @pl.when(far_here == j % 2)
             def _(j=j):
                 ring(FAR - 1, j).wait_recv()
                 add(FAR, j, jnp.dot(left(j), ring_in[FAR - 1, j // 2], preferred_element_type=F32), j < 2)
-        if t == 5:
-            for d in (0, 1, 2):
-                ship(d)
-        if t == 6:
-            ship(3)
-            for d in (0, 1, 2):
-                collect(d)
     ship(FAR)
-    collect(3)
-    collect(FAR)
+    for d in range(FAR + 1):
+        collect(d)
 
     delta = lax.rem(p - z + NZ, NZ)
     mom_ref[...] = jnp.zeros_like(mom_ref)

time: 74 us -> 67.8 us (0.916)
  Pallas kernels: 67.1 us -> 60.2 us
    pallas_call x1, Pallas kernels: 67.1 us -> 60.2 us  [on_device(): pl.pallas_call(kernel, out_shape=(jax.ShapeDtypeStruct((paths, CP), BF),...]
where the time goes in v3:
time: 67.8 us; the launch traced here: 66.8 us
  Pallas kernels  60.2 us (89%)
  local copies, waits for them, and re-layouts  5.15 us (8%)
  other arithmetic  0.75 us (1%)
  between operations  0.68 us (1%)
    pallas_call x1, Pallas kernels, on_device(): pl.pallas_call(kernel, out_shape=(jax.ShapeDtypeStruct((paths, CP), BF),...  60.2 us
    unnamed x8, local copies, waits for them, and re-layouts  2.81 us
    another operation x4, local copies, waits for them, and re-layouts, on_device(): jnp.stack([notional, strike, curvature, local])  2.09 us

profile of v3, /device:TPU:4, one launch (start us, length us, event | category | flops | bytes accessed | tf_op | source)
XLA Modules:
  0.0 66.8 jit_solution(15083124998766842439)
XLA Ops:
  0.6 0.0 copy-start
  0.6 0.8 %fusion.1 = bf16[2048]{0:T(1024)(128)(2,1)S(1)} fusion(s32[2048]{0:T(1024)} %param.11), kind=kLoop, calls=%fused_computation.4 | loop fusion | flops 24576 | bytes 12288 | tf_op jit(solution)/shard_map/convert_element_type | solution.py:305
  1.4 0.7 %stack.12 = bf16[1,2048]{1,0:T(2,128)(2,1)S(1)} reshape(bf16[2048]{0:T(1024)(128)(2,1)} %param.8) | data formatting | bytes 8192 | tf_op jit(solution)/shard_map/stack | solution.py:307
  2.1 0.7 %stack.13 = bf16[1,2048]{1,0:T(2,128)(2,1)S(1)} reshape(bf16[2048]{0:T(1024)(128)(2,1)} %param.9) | data formatting | bytes 8192 | tf_op jit(solution)/shard_map/stack | solution.py:307
  2.8 0.7 %stack.14 = bf16[1,2048]{1,0:T(2,128)(2,1)S(1)} reshape(bf16[2048]{0:T(1024)(128)(2,1)} %param.10) | data formatting | bytes 8192 | tf_op jit(solution)/shard_map/stack | solution.py:307
  3.5 0.0 copy-start.2
  3.5 0.2 concatenate.3.term_ref
  3.8 0.0 copy-done
  3.8 0.4 copy-done.2
  4.2 0.0 copy-start.1
  4.2 0.9 %copy-done.1 = bf16[64,1536]{1,0:T(8,128)(2,1)S(1)} copy-done((bf16[64,1536]{1,0:T(8,128)(2,1)S(1)}, bf16[64,1536]{1,0:T(8,128)(2,1)}, u32[]{:S(2)}) %copy-start.1) | copy-done | bytes 196632
  5.1 60.2 %shard_map.77 = (bf16[1536,128]{1,0:T(8,128)(2,1)S(1)}, f32[4,128,128]{2,1,0:T(8,128)S(1)}) custom-call(bf16[64,1536]{1,0:T(8,128)(2,1)S(1)} %copy-done.1, bf16[64,2048]{1,0:T(8,128)(2,1)S(1)} %copy-done, bf16[16,2048]{1,0:T(8,128)(2,1)S(1)} %concatenate.3.term_ref, s32[1,2048]{1,0:T(1,128)S(1)} %bitcast.3), custom_call_target="tpu_custom_call" | custom-call | tf_op jit(solution)/shard_map/pallas_call | solution.py:310
  65.3 0.7 %copy.10 = bf16[1536,128]{1,0:T(8,128)(2,1)} copy(bf16[1536,128]{1,0:T(8,128)(2,1)S(1)} %get-tuple-element.8) | data formatting | bytes 786432
  66.1 0.7 %copy.11 = f32[512,128]{1,0:T(8,128)} copy(f32[512,128]{1,0:T(8,128)S(1)} %bitcast.2) | data formatting | bytes 524288
  (2 shorter events, 0.0 us)
Async XLA Ops:
  0.6 3.1 %copy-start = (bf16[64,2048]{1,0:T(8,128)(2,1)S(1)}, bf16[64,2048]{1,0:T(8,128)(2,1)}, u32[]{:S(2)}) copy-start(bf16[64,2048]{1,0:T(8,128)(2,1)} %load_ref.1) | copy-start | bytes 786436
  3.5 0.7 %copy-start.2 = (s32[2048]{0:T(1024)S(1)}, s32[2048]{0:T(1024)}, u32[]{:S(2)}) copy-start(s32[2048]{0:T(1024)} %param.11) | copy-start | bytes 24580
  4.2 0.9 %copy-start.1 = (bf16[64,1536]{1,0:T(8,128)(2,1)S(1)}, bf16[64,1536]{1,0:T(8,128)(2,1)}, u32[]{:S(2)}) copy-start(bf16[64,1536]{1,0:T(8,128)(2,1)} %fac_ref.1) | copy-start | bytes 589828

commit v4 on v3

--- a/solution.py
+++ b/solution.py
@@ -24,7 +24,7 @@
 
 
 def kernel(fac_ref, load_ref, term_ref, id_ref, exp_ref, mom_ref,
-           desc, pack, trades, hot, ft, net, own, at, ring_in, acc, rsb, rr, keep, turn, fa, fb,
+           desc, pack, trades, hot, ft, net, own, at, ring_in, acc, rsb, mid, rr, keep, turn, fa, fb,
            s1, r1, s2, r2, sy, ry, sz, rz, srs, rrs, sa, ra, sb, rb):
     p = lax.axis_index("paths")
     c = lax.axis_index("cpty")
@@ -104,11 +104,30 @@
         @pl.when(k != c)
         def _(arrive=arrive):
             arrive.wait_recv()
-    spread = []
-    for r in range(1, NP):
-        copy = remote(trades.at[p], trades.at[p], s2.at[r], r2.at[r], lax.rem(p + r, NP), c)
+    sends = []
+
+    def go(copy):
         copy.start()
-        spread.append(copy)
+        sends.append(copy)
+
+    x_ahead, x_back, x_far = lax.rem(x - sign + NX, NX), lax.rem(x + sign + NX, NX), lax.rem(x + 2, NX)
+    partner = 2 * x + 1 - core
+    mates = [2 * i + core for i in (x, x_back, x_ahead, x_far)]
+    others = [2 * i + 1 - core for i in (x, x_ahead, x_back, x_far)]
+
+    def across(i):
+        return remote(trades.at[mates[i]], trades.at[mates[i]], s2.at[i], r2.at[i], partner, c)
+
+    def across_wait(i):
+        remote(trades.at[others[i]], trades.at[others[i]], s2.at[i], r2.at[i], partner, c).wait_recv()
+
+    def along(i):
+        src = mates[1] if i == 3 else p
+        dst = mates[1] if i == 2 else mates[2]
+        return remote(trades.at[src], trades.at[src], s2.at[NX + i], r2.at[NX + i], dst, c)
+
+    def along_wait(i):
+        remote(trades.at[mates[i]], trades.at[mates[i]], s2.at[NX + i], r2.at[NX + i], partner, c).wait_recv()
 
     def tile_of(pp):
         t = trades[pp]
@@ -121,12 +140,6 @@
         value = terms[0:1, :] * (lin + terms[2:3, :] * jnp.tanh(lin - terms[1:2, :]))
         return lax.dot_general(value.astype(BF), hot[pp], NT, preferred_element_type=F32)
 
-    sends = []
-
-    def go(copy):
-        copy.start()
-        sends.append(copy)
-
     def ring(s, j):
         src = own.at[j] if s == 0 else ring_in.at[s - 1, j]
         slot = j if s < FAR - 1 else j // 2
@@ -150,14 +163,34 @@
     def left(j):
         return at[j].reshape(NY * CP, rows)
 
+    def dots(d, j):
+        right = own[j] if d == 0 else ring_in[d - 1, j]
+        add(d, j, jnp.dot(left(j), right, preferred_element_type=F32), j == 0)
+
     def cell(d):
         return lax.rem(z + sign * d + NZ, NZ)
 
+    near_x, wide_x = x + 1 - 2 * (x % 2), NX - 1 - x
+    first_x = near_x + core * (wide_x - near_x)
+    second_x = wide_x + core * (near_x - wide_x)
+    passed = 6 - x - first_x - second_x
+
+    def tile(d, i):
+        return acc[d, pl.ds(pl.multiple_of(i * CP, CP), CP), :]
+
+    def reduce(d, i):
+        src, to = ((rsb.at[d, first_x], first_x), (rsb.at[d, passed], first_x), (mid.at[d], second_x))[i]
+        return remote(src, rr.at[d, i], srs.at[d, i], rrs.at[d, i], 2 * to + core, c)
+
     def ship(d):
         rsb[d] = acc[d].reshape(NY, CP, CP).astype(BF)
-        for r in range(1, NX):
-            xx = lax.rem(x + r, NX)
-            go(remote(rsb.at[d, xx], rr.at[d, r], srs.at[d, r], rrs.at[d, r], 2 * xx + core, c))
+        go(reduce(d, 1))
+        go(reduce(d, 0))
+
+    def pass_on(d):
+        reduce(d, 1).wait_recv()
+        mid[d] = (tile(d, second_x) + rr[d, 1].astype(F32)).astype(BF)
+        go(reduce(d, 2))
 
     def turned(d):
         return remote(turn.at[d], fa.at[core, y], sa.at[d], ra.at[core, y], cell(d), z * NY + x)
@@ -169,11 +202,9 @@
         return remote(keep.at[d], fb.at[core, x], sb.at[d], rb.at[core, x], z, cell(d) * NY + y)
 
     def collect(d):
-        whole = acc[d, pl.ds(pl.multiple_of(x * CP, CP), CP), :]
-        for r in range(1, NX):
-            src = lax.rem(x - r + NX, NX)
-            remote(rsb.at[d, src], rr.at[d, r], srs.at[d, r], rrs.at[d, r], 2 * src + core, c).wait_recv()
-            whole = whole + rr[d, r].astype(F32)
+        reduce(d, 0).wait_recv()
+        reduce(d, 2).wait_recv()
+        whole = tile(d, x) + rr[d, 0].astype(F32) + rr[d, 2].astype(F32)
         whole = whole * (1.0 / (paths * NP))
         if d > 0:
             keep[d] = whole.astype(BF)
@@ -193,22 +224,41 @@
             j = t
             net[...] = jnp.zeros_like(net)
 
-            def body(r, _):
-                pp = lax.rem(p + r, NP)
-                if j == 0:
-                    @pl.when(r > 0)
-                    def _():
-                        src = lax.rem(p - r + NP, NP)
-                        remote(trades.at[src], trades.at[src], s2.at[r], r2.at[r], src, c).wait_recv()
-
-                    pp = lax.rem(p - r + NP, NP)
-                    t4 = trades[pp]
-                    label = jnp.concatenate([t4[i][F:ROWS, :] for i in range(4)], axis=1).astype(F32)[3:4, :]
-                    hot[pp] = (lax.broadcasted_iota(jnp.int32, (CP, 4 * SLOT), 0).astype(F32) == label).astype(F32).astype(BF)
-                net[...] += price(j, pp)
-                return 0
-
-            lax.fori_loop(0, NP, body, 0, unroll=1 if j == 0 else NP)
+            def take(pp):
+                t4 = trades[pp]
+                label = jnp.concatenate([t4[i][F:ROWS, :] for i in range(4)], axis=1).astype(F32)[3:4, :]
+                hot[pp] = (lax.broadcasted_iota(jnp.int32, (CP, 4 * SLOT), 0).astype(F32) == label).astype(F32).astype(BF)
+                net[...] += price(0, pp)
+
+            if j == 0:
+                go(along(1))
+                go(along(2))
+                go(across(0))
+                take(p)
+                across_wait(0)
+                take(others[0])
+                along_wait(1)
+                go(along(3))
+                go(across(1))
+                along_wait(2)
+                go(across(2))
+                take(mates[1])
+                take(mates[2])
+                across_wait(1)
+                take(others[1])
+                across_wait(2)
+                take(others[2])
+                along_wait(3)
+                go(across(3))
+                take(mates[3])
+                across_wait(3)
+                take(others[3])
+            else:
+                def body(r, _):
+                    net[...] += price(j, r)
+                    return 0
+
+                lax.fori_loop(0, NP, body, 0, unroll=NP)
             block_f = jnp.maximum(net[...], 0.0)
             block_b = block_f.astype(BF)
             own[j] = block_b
@@ -217,6 +267,11 @@
             go(ring(0, j))
             go(side(j, 0))
             go(side(j, 1))
+        j = t - 2
+        if 0 <= j < CH - 1:
+            side_wait(j, 0)
+            go(side(j, 2))
+            side_wait(j, 1)
         for s in range(1, FAR):
             j = t - 1 - s
             if 0 <= j < CH:
@@ -229,34 +284,45 @@
                     @pl.when(far_ahead == j % 2)
                     def _(copy=copy):
                         copy.start()
-        j = t - 2
-        if 0 <= j < CH:
-            side_wait(j, 0)
-            go(side(j, 2))
-            side_wait(j, 1)
+        if t == CH:
+            side_wait(CH - 1, 0)
+            go(side(CH - 1, 2))
+            side_wait(CH - 1, 1)
         j = t - 3
-        if 0 <= j < CH:
+        if 0 <= j < CH - 1:
             side_wait(j, 2)
-            add(0, j, jnp.dot(left(j), own[j], preferred_element_type=F32), j == 0)
-            for d in (1, 2):
-                add(d, j, jnp.dot(left(j), ring_in[d - 1, j], preferred_element_type=F32), j == 0)
-            if j == CH - 1:
-                for d in (0, 1, 2):
-                    ship(d)
+            for d in (0, 1, 2):
+                dots(d, j)
         j = t - 4
         if 0 <= j < CH:
-            add(3, j, jnp.dot(left(j), ring_in[2, j], preferred_element_type=F32), j == 0)
-            if j == CH - 1:
-                ship(3)
+            dots(3, j)
         j = t - 1 - FAR
         if 0 <= j < CH:
             @pl.when(far_here == j % 2)
             def _(j=j):
                 ring(FAR - 1, j).wait_recv()
                 add(FAR, j, jnp.dot(left(j), ring_in[FAR - 1, j // 2], preferred_element_type=F32), j < 2)
+        if t == CH + 1:
+            side_wait(CH - 1, 2)
+            for d in (0, 1):
+                dots(d, CH - 1)
+                ship(d)
+        if t == CH + 2:
+            dots(2, CH - 1)
+            ship(2)
+        if t == CH + 3:
+            ship(3)
+            pass_on(0)
+            pass_on(1)
     ship(FAR)
-    for d in range(FAR + 1):
-        collect(d)
+    collect(0)
+    pass_on(2)
+    collect(1)
+    pass_on(3)
+    collect(2)
+    pass_on(FAR)
+    collect(3)
+    collect(FAR)
 
     delta = lax.rem(p - z + NZ, NZ)
     mom_ref[...] = jnp.zeros_like(mom_ref)
@@ -283,8 +349,6 @@
         @pl.when(k != c)
         def _(copy=copy):
             copy.wait_send()
-    for copy in spread:
-        copy.wait_send()
     for copy in sends:
         copy.wait_send()
     for j in range(CH):
@@ -324,14 +388,15 @@
             pltpu.VMEM((FAR, CH, rows, CP), BF),
             pltpu.VMEM((FAR + 1, NY * CP, CP), F32),
             pltpu.VMEM((FAR + 1, NY, CP, CP), BF),
-            pltpu.VMEM((FAR + 1, NX, CP, CP), BF),
+            pltpu.VMEM((FAR + 1, CP, CP), BF),
+            pltpu.VMEM((FAR + 1, 3, CP, CP), BF),
             pltpu.VMEM((FAR + 1, CP, CP), BF),
             pltpu.VMEM((FAR + 1, CP, CP), BF),
             pltpu.VMEM((2, NY, CP, CP), BF),
             pltpu.VMEM((2, NX, CP, CP), BF),
             dma((4,)), dma((4,)), dma((NP,)), dma((NP,)),
             dma((CH, 3)), dma((CH, 3)), dma((FAR, CH)), dma((FAR, CH)),
-            dma((FAR + 1, NX)), dma((FAR + 1, NX)),
+            dma((FAR + 1, 3)), dma((FAR + 1, 3)),
             dma((FAR + 1,)), dma((2, NY)), dma((FAR + 1,)), dma((2, NX)),
         ],
         compiler_params=pltpu.CompilerParams(

time: 67.8 us -> 71.3 us (1.052); the launches traced: 66.8 us -> 71 us
  Pallas kernels: 60.2 us -> 64.5 us
    pallas_call x1, Pallas kernels: 60.2 us -> 64.5 us  [on_device(): pl.pallas_call(kernel, out_shape=(jax.ShapeDtypeStruct((paths, CP), BF),...]
where the time goes in v4:
time: 71.3 us; the launch traced here: 71 us
  Pallas kernels  64.5 us (90%)
  local copies, waits for them, and re-layouts  5.15 us (7%)
  other arithmetic  0.75 us (1%)
    pallas_call x1, Pallas kernels, on_device(): pl.pallas_call(kernel, out_shape=(jax.ShapeDtypeStruct((paths, CP), BF),...  64.5 us
    unnamed x8, local copies, waits for them, and re-layouts  2.81 us
    another operation x4, local copies, waits for them, and re-layouts, on_device(): jnp.stack([notional, strike, curvature, local])  2.09 us

profile of v4, /device:TPU:4, one launch (start us, length us, event | category | flops | bytes accessed | tf_op | source)
XLA Modules:
  0.0 71.0 jit_solution(10409473894841370386)
XLA Ops:
  0.6 0.0 copy-start
  0.6 0.8 %fusion.1 = bf16[2048]{0:T(1024)(128)(2,1)S(1)} fusion(s32[2048]{0:T(1024)} %param.11), kind=kLoop, calls=%fused_computation.4 | loop fusion | flops 24576 | bytes 12288 | tf_op jit(solution)/shard_map/convert_element_type | solution.py:369
  1.4 0.7 stack.12
  2.1 0.7 stack.13
  2.8 0.7 stack.14
  3.5 0.0 copy-start.2
  3.5 0.2 concatenate.3.term_ref
  3.8 0.0 copy-done
  3.8 0.4 copy-done.2
  4.2 0.0 copy-start.1
  4.2 0.9 %copy-done.1 = bf16[64,1536]{1,0:T(8,128)(2,1)S(1)} copy-done((bf16[64,1536]{1,0:T(8,128)(2,1)S(1)}, bf16[64,1536]{1,0:T(8,128)(2,1)}, u32[]{:S(2)}) %copy-start.1) | copy-done | bytes 196632
  5.1 64.5 %shard_map.77 = (bf16[1536,128]{1,0:T(8,128)(2,1)S(1)}, f32[4,128,128]{2,1,0:T(8,128)S(1)}) custom-call(bf16[64,1536]{1,0:T(8,128)(2,1)S(1)} %copy-done.1, bf16[64,2048]{1,0:T(8,128)(2,1)S(1)} %copy-done, bf16[16,2048]{1,0:T(8,128)(2,1)S(1)} %concatenate.3.term_ref, s32[1,2048]{1,0:T(1,128)S(1)} %bitcast.3), custom_call_target="tpu_custom_call" | custom-call | tf_op jit(solution)/shard_map/pallas_call | solution.py:374
  69.6 0.7 %copy.10 = bf16[1536,128]{1,0:T(8,128)(2,1)} copy(bf16[1536,128]{1,0:T(8,128)(2,1)S(1)} %get-tuple-element.8) | data formatting | bytes 786432
  70.3 0.7 copy.11
  (2 shorter events, 0.0 us)
Async XLA Ops:
  0.6 3.1 %copy-start = (bf16[64,2048]{1,0:T(8,128)(2,1)S(1)}, bf16[64,2048]{1,0:T(8,128)(2,1)}, u32[]{:S(2)}) copy-start(bf16[64,2048]{1,0:T(8,128)(2,1)} %load_ref.1) | copy-start | bytes 786436
  3.5 0.7 copy-start.2
  4.2 0.9 %copy-start.1 = (bf16[64,1536]{1,0:T(8,128)(2,1)S(1)}, bf16[64,1536]{1,0:T(8,128)(2,1)}, u32[]{:S(2)}) copy-start(bf16[64,1536]{1,0:T(8,128)(2,1)} %fac_ref.1) | copy-start | bytes 589828

commit v5 on v4

--- a/solution.py
+++ b/solution.py
@@ -11,7 +11,10 @@
 ROWS = 80
 SLOT = 128
 F = 64
-CH = 4
+SIZES = (512, 512, 384, 128)
+STARTS = (0, 512, 1024, 1408)
+CH = len(SIZES)
+FAR_SIDE = (0, 1, 1, 0)
 BF, F32 = jnp.bfloat16, jnp.float32
 NT = (((1,), (1,)), ((), ()))
 
@@ -23,14 +26,15 @@
     )
 
 
-def kernel(fac_ref, load_ref, term_ref, id_ref, exp_ref, mom_ref,
-           desc, pack, trades, hot, ft, net, own, at, ring_in, acc, rsb, mid, rr, keep, turn, fa, fb,
+def kernel(fac_hbm, load_hbm, not_hbm, str_hbm, cur_hbm, id_hbm, exp_ref, mom_ref,
+           fac_ref, term_in, id_ref, desc, pack, trades, hot, ft, net, own, at0, at1, at2, at3,
+           ring_in, acc, rsb, mid, rr, keep, turn, fa, fb, sin,
            s1, r1, s2, r2, sy, ry, sz, rz, srs, rrs, sa, ra, sb, rb):
     p = lax.axis_index("paths")
     c = lax.axis_index("cpty")
     z, y = c // NY, c % NY
+    at = (at0, at1, at2, at3)
     paths = fac_ref.shape[1]
-    rows = paths // CH
     count = id_ref.shape[1]
     first = lax.rem(p - c + 32, 8)
     targets = [first + 8 * i for i in range(4)]
@@ -57,8 +61,16 @@
     for r in range(1, NY):
         greet(p, z * NY + lax.rem(y + r, NY))
 
-    desc[0:F, :] = load_ref[...]
-    desc[F:ROWS, :] = term_ref[...]
+    loads = [
+        pltpu.make_async_copy(src, dst, sin.at[i])
+        for i, (src, dst) in enumerate((
+            (id_hbm, id_ref), (not_hbm, term_in.at[0]), (str_hbm, term_in.at[1]),
+            (cur_hbm, term_in.at[2]), (load_hbm, desc.at[0:F, :]), (fac_hbm, fac_ref)))
+    ]
+    for copy in loads:
+        copy.start()
+    loads[0].wait()
+
     ids = id_ref[...]
     owner = ids // CP
     block = 256
@@ -75,6 +87,15 @@
     rank = jnp.concatenate(ranks, axis=1).astype(jnp.int32)
     mine = lax.rem(owner + c, 8) == p
     code = jnp.where(mine, (owner // 8) * SLOT + rank, -1)
+    for copy in loads[1:5]:
+        copy.wait()
+    line = lax.broadcasted_iota(jnp.int32, (ROWS - F, count), 0)
+    extra = jnp.where(line == 3, (ids % CP).astype(F32), 0.0)
+    for i in range(3):
+        cells = term_in[i].astype(F32)
+        flat = jnp.concatenate([cells[k:k + 1, :] for k in range(count // CP)], axis=1)
+        extra = jnp.where(line == i, flat, extra)
+    desc[F:ROWS, :] = extra.astype(BF)
     total = jnp.zeros((ROWS, 4 * SLOT), F32)
     step = 512
     for b in range(count // step):
@@ -83,7 +104,6 @@
         total = total + lax.dot_general(desc[:, cols], chosen, NT, preferred_element_type=F32)
     for i in range(4):
         pack[i] = total[:, i * SLOT:(i + 1) * SLOT].astype(BF)
-    ft[...] = jnp.transpose(fac_ref[...].astype(F32)).astype(BF)
 
     pl.semaphore_wait(barrier, NP - 1 + 2 + NY - 1 + 4 - (lax.rem(2 * c, 8) == p).astype(jnp.int32))
 
@@ -98,6 +118,8 @@
         @pl.when(k == c)
         def _(i=i):
             trades[p, place] = pack[i]
+    loads[5].wait()
+    ft[...] = jnp.transpose(fac_ref[...].astype(F32)).astype(BF)
     for i, k in enumerate(targets):
         arrive = remote(pack.at[i], trades.at[p, i], s1.at[i], r1.at[i], p, k)
 
@@ -129,6 +151,12 @@
     def along_wait(i):
         remote(trades.at[mates[i]], trades.at[mates[i]], s2.at[NX + i], r2.at[NX + i], partner, c).wait_recv()
 
+    def span(j):
+        return slice(STARTS[j], STARTS[j] + SIZES[j])
+
+    def cut(j):
+        return pl.ds(STARTS[j], SIZES[j])
+
     def tile_of(pp):
         t = trades[pp]
         return jnp.concatenate([t[i] for i in range(4)], axis=1)
@@ -136,23 +164,22 @@
     def price(j, pp):
         full = tile_of(pp)
         terms = full[F:ROWS, :].astype(F32)
-        lin = jnp.dot(ft[j * rows:(j + 1) * rows, :], full[0:F, :], preferred_element_type=F32)
+        lin = jnp.dot(ft[span(j), :], full[0:F, :], preferred_element_type=F32)
         value = terms[0:1, :] * (lin + terms[2:3, :] * jnp.tanh(lin - terms[1:2, :]))
         return lax.dot_general(value.astype(BF), hot[pp], NT, preferred_element_type=F32)
 
     def ring(s, j):
-        src = own.at[j] if s == 0 else ring_in.at[s - 1, j]
-        slot = j if s < FAR - 1 else j // 2
-        return remote(src, ring_in.at[s, slot], sz.at[s, slot], rz.at[s, slot], p, ahead * NY + y)
+        src = own.at[cut(j)] if s == 0 else ring_in.at[s - 1, cut(j)]
+        return remote(src, ring_in.at[s, cut(j)], sz.at[s, j], rz.at[s, j], p, ahead * NY + y)
 
     def side(j, way):
         origin = y if way < 2 else y_back
         target = y_back if way == 1 else y_ahead
-        return remote(at.at[j, origin], at.at[j, origin], sy.at[j, way], ry.at[j, way], p, z * NY + target)
+        return remote(at[j].at[origin], at[j].at[origin], sy.at[j, way], ry.at[j, way], p, z * NY + target)
 
     def side_wait(j, way):
         origin = (y_back, y_ahead, lax.rem(y + 2, NY))[way]
-        remote(at.at[j, origin], at.at[j, origin], sy.at[j, way], ry.at[j, way], p, z * NY + y_back).wait_recv()
+        remote(at[j].at[origin], at[j].at[origin], sy.at[j, way], ry.at[j, way], p, z * NY + y_back).wait_recv()
 
     def add(d, j, value, start):
         if start:
@@ -161,11 +188,11 @@
             acc[d] += value
 
     def left(j):
-        return at[j].reshape(NY * CP, rows)
-
-    def dots(d, j):
-        right = own[j] if d == 0 else ring_in[d - 1, j]
-        add(d, j, jnp.dot(left(j), right, preferred_element_type=F32), j == 0)
+        return at[j][...].reshape(NY * CP, SIZES[j])
+
+    def dots(d, j, start=None):
+        right = own[span(j), :] if d == 0 else ring_in[d - 1, span(j), :]
+        add(d, j, jnp.dot(left(j), right, preferred_element_type=F32), j == 0 if start is None else start)
 
     def cell(d):
         return lax.rem(z + sign * d + NZ, NZ)
@@ -179,13 +206,17 @@
         return acc[d, pl.ds(pl.multiple_of(i * CP, CP), CP), :]
 
     def reduce(d, i):
-        src, to = ((rsb.at[d, first_x], first_x), (rsb.at[d, passed], first_x), (mid.at[d], second_x))[i]
+        if d < 3:
+            src, to = ((rsb.at[d, first_x], first_x), (rsb.at[d, passed], first_x), (mid.at[d], second_x))[i]
+        else:
+            to = lax.rem(x + i + 1, NX)
+            src = rsb.at[d, to]
         return remote(src, rr.at[d, i], srs.at[d, i], rrs.at[d, i], 2 * to + core, c)
 
     def ship(d):
         rsb[d] = acc[d].reshape(NY, CP, CP).astype(BF)
-        go(reduce(d, 1))
-        go(reduce(d, 0))
+        for i in ((1, 0) if d < 3 else (1, 0, 2)):
+            go(reduce(d, i))
 
     def pass_on(d):
         reduce(d, 1).wait_recv()
@@ -202,9 +233,10 @@
         return remote(keep.at[d], fb.at[core, x], sb.at[d], rb.at[core, x], z, cell(d) * NY + y)
 
     def collect(d):
-        reduce(d, 0).wait_recv()
-        reduce(d, 2).wait_recv()
-        whole = tile(d, x) + rr[d, 0].astype(F32) + rr[d, 2].astype(F32)
+        whole = tile(d, x)
+        for i in ((0, 2) if d < 3 else (0, 1, 2)):
+            reduce(d, i).wait_recv()
+            whole = whole + rr[d, i].astype(F32)
         whole = whole * (1.0 / (paths * NP))
         if d > 0:
             keep[d] = whole.astype(BF)
@@ -222,56 +254,51 @@
     for t in range(CH + FAR + 1):
         if t < CH:
             j = t
-            net[...] = jnp.zeros_like(net)
-
-            def take(pp):
-                t4 = trades[pp]
-                label = jnp.concatenate([t4[i][F:ROWS, :] for i in range(4)], axis=1).astype(F32)[3:4, :]
-                hot[pp] = (lax.broadcasted_iota(jnp.int32, (CP, 4 * SLOT), 0).astype(F32) == label).astype(F32).astype(BF)
-                net[...] += price(0, pp)
+            here = net.at[0:SIZES[j], :]
+
+            def take(*group):
+                for pp in group:
+                    t4 = trades[pp]
+                    label = jnp.concatenate([t4[i][F:ROWS, :] for i in range(4)], axis=1).astype(F32)[3:4, :]
+                    hot[pp] = (lax.broadcasted_iota(jnp.int32, (CP, 4 * SLOT), 0).astype(F32) == label).astype(F32).astype(BF)
+                here[...] += sum(price(0, pp) for pp in group)
 
             if j == 0:
                 go(along(1))
                 go(along(2))
                 go(across(0))
-                take(p)
+                here[...] = jnp.zeros_like(here)
                 across_wait(0)
-                take(others[0])
+                take(p, others[0])
                 along_wait(1)
                 go(along(3))
                 go(across(1))
                 along_wait(2)
                 go(across(2))
-                take(mates[1])
-                take(mates[2])
+                take(mates[1], mates[2])
                 across_wait(1)
-                take(others[1])
                 across_wait(2)
-                take(others[2])
+                take(others[1], others[2])
                 along_wait(3)
                 go(across(3))
-                take(mates[3])
                 across_wait(3)
-                take(others[3])
+                take(mates[3], others[3])
             else:
+                here[...] = jnp.zeros_like(here)
+
                 def body(r, _):
-                    net[...] += price(j, r)
+                    here[...] += price(j, r)
                     return 0
 
                 lax.fori_loop(0, NP, body, 0, unroll=NP)
-            block_f = jnp.maximum(net[...], 0.0)
+            block_f = jnp.maximum(here[...], 0.0)
             block_b = block_f.astype(BF)
-            own[j] = block_b
-            exp_ref[j * rows:(j + 1) * rows, :] = block_b
-            at[j, y] = jnp.transpose(block_f).astype(BF)
+            own[span(j), :] = block_b
+            exp_ref[span(j), :] = block_b
+            at[j][y] = jnp.transpose(block_f).astype(BF)
             go(ring(0, j))
             go(side(j, 0))
             go(side(j, 1))
-        j = t - 2
-        if 0 <= j < CH - 1:
-            side_wait(j, 0)
-            go(side(j, 2))
-            side_wait(j, 1)
         for s in range(1, FAR):
             j = t - 1 - s
             if 0 <= j < CH:
@@ -281,13 +308,13 @@
                 else:
                     copy = ring(s, j)
 
-                    @pl.when(far_ahead == j % 2)
+                    @pl.when(far_ahead == FAR_SIDE[j])
                     def _(copy=copy):
                         copy.start()
-        if t == CH:
-            side_wait(CH - 1, 0)
-            go(side(CH - 1, 2))
-            side_wait(CH - 1, 1)
+        for j in {2: (0,), 3: (1,), 4: (2, 3)}.get(t, ()):
+            side_wait(j, 0)
+            go(side(j, 2))
+            side_wait(j, 1)
         j = t - 3
         if 0 <= j < CH - 1:
             side_wait(j, 2)
@@ -298,10 +325,10 @@
             dots(3, j)
         j = t - 1 - FAR
         if 0 <= j < CH:
-            @pl.when(far_here == j % 2)
+            @pl.when(far_here == FAR_SIDE[j])
             def _(j=j):
                 ring(FAR - 1, j).wait_recv()
-                add(FAR, j, jnp.dot(left(j), ring_in[FAR - 1, j // 2], preferred_element_type=F32), j < 2)
+                dots(FAR, j, j < 2)
         if t == CH + 1:
             side_wait(CH - 1, 2)
             for d in (0, 1):
@@ -314,15 +341,10 @@
             ship(3)
             pass_on(0)
             pass_on(1)
+            pass_on(2)
     ship(FAR)
-    collect(0)
-    pass_on(2)
-    collect(1)
-    pass_on(3)
-    collect(2)
-    pass_on(FAR)
-    collect(3)
-    collect(FAR)
+    for d in range(FAR + 1):
+        collect(d)
 
     delta = lax.rem(p - z + NZ, NZ)
     mom_ref[...] = jnp.zeros_like(mom_ref)
@@ -354,7 +376,7 @@
     for j in range(CH):
         copy = ring(FAR - 1, j)
 
-        @pl.when(far_ahead == j % 2)
+        @pl.when(far_ahead == FAR_SIDE[j])
         def _(copy=copy):
             copy.wait_send()
     for d in range(FAR + 1):
@@ -365,27 +387,26 @@
 
 def on_device(factors, loadings, notional, strike, curvature, trade_cpty):
     count, paths = loadings.shape[1], factors.shape[1]
-    rows = paths // CH
-    local = (trade_cpty % CP).astype(BF)
-    terms = jnp.concatenate(
-        [jnp.stack([notional, strike, curvature, local]), jnp.zeros((ROWS - F - 4, count), BF)], axis=0)
     vmem = pl.BlockSpec(memory_space=pltpu.VMEM)
     dma = pltpu.SemaphoreType.DMA
     exposure, moment = pl.pallas_call(
         kernel,
         out_shape=(jax.ShapeDtypeStruct((paths, CP), BF), jax.ShapeDtypeStruct((NY, CP, CP), F32)),
-        in_specs=[vmem] * 4,
+        in_specs=[pl.BlockSpec(memory_space=pl.ANY)] * 6,
         out_specs=(vmem, vmem),
         scratch_shapes=[
+            pltpu.VMEM((F, paths), BF),
+            pltpu.VMEM((3, count // CP, CP), BF),
+            pltpu.VMEM((1, count), jnp.int32),
             pltpu.VMEM((ROWS, count), BF),
             pltpu.VMEM((4, ROWS, SLOT), BF),
             pltpu.VMEM((NP, 4, ROWS, SLOT), BF),
             pltpu.VMEM((NP, CP, 4 * SLOT), BF),
             pltpu.VMEM((paths, F), BF),
-            pltpu.VMEM((rows, CP), F32),
-            pltpu.VMEM((CH, rows, CP), BF),
-            pltpu.VMEM((CH, NY, CP, rows), BF),
-            pltpu.VMEM((FAR, CH, rows, CP), BF),
+            pltpu.VMEM((max(SIZES), CP), F32),
+            pltpu.VMEM((paths, CP), BF),
+            *[pltpu.VMEM((NY, CP, n), BF) for n in SIZES],
+            pltpu.VMEM((FAR, paths, CP), BF),
             pltpu.VMEM((FAR + 1, NY * CP, CP), F32),
             pltpu.VMEM((FAR + 1, NY, CP, CP), BF),
             pltpu.VMEM((FAR + 1, CP, CP), BF),
@@ -394,14 +415,15 @@
             pltpu.VMEM((FAR + 1, CP, CP), BF),
             pltpu.VMEM((2, NY, CP, CP), BF),
             pltpu.VMEM((2, NX, CP, CP), BF),
-            dma((4,)), dma((4,)), dma((NP,)), dma((NP,)),
+            dma((6,)), dma((4,)), dma((4,)), dma((NP,)), dma((NP,)),
             dma((CH, 3)), dma((CH, 3)), dma((FAR, CH)), dma((FAR, CH)),
             dma((FAR + 1, 3)), dma((FAR + 1, 3)),
             dma((FAR + 1,)), dma((2, NY)), dma((FAR + 1,)), dma((2, NX)),
         ],
         compiler_params=pltpu.CompilerParams(
-            collective_id=0, has_side_effects=True, vmem_limit_bytes=50 * 1024 * 1024),
-    )(factors, loadings, terms, trade_cpty[None, :])
+            collective_id=0, has_side_effects=True, vmem_limit_bytes=67043328),
+    )(factors, loadings, *[a.reshape(count // CP, CP) for a in (notional, strike, curvature)],
+      trade_cpty[None, :])
     return exposure, moment.reshape(NY * CP, CP)
 
 

time: 71.3 us -> 66.5 us (0.933)
  local copies, waits for them, and re-layouts: 5.15 us -> 2.52 us
  Pallas kernels: 64.5 us -> 63.3 us
  other arithmetic: 0.75 us -> 0 us
    another operation x4 -> x0, local copies, waits for them, and re-layouts: 2.09 us -> none  [on_device(): jnp.stack([notional, strike, curvature, local])]
    pallas_call x1, Pallas kernels: 64.5 us -> 63.3 us  [on_device(): pl.pallas_call(kernel, out_shape=(jax.ShapeDtypeStruct((paths, CP), BF),...]
    convert_element_type x1 -> x0, other arithmetic: 0.75 us -> none  [on_device(): local = (trade_cpty % CP).astype(BF)]
    unnamed x8 -> x4, local copies, waits for them, and re-layouts: 2.81 us -> 2.52 us
where the time goes in v5:
time: 66.5 us; the launch traced here: 66.4 us
  Pallas kernels  63.3 us (95%)
  local copies, waits for them, and re-layouts  2.52 us (4%)
    pallas_call x1, Pallas kernels, on_device(): pl.pallas_call(kernel, out_shape=(jax.ShapeDtypeStruct((paths, CP), BF),...  63.3 us
    unnamed x4, local copies, waits for them, and re-layouts  2.52 us

profile of v5, /device:TPU:4, one launch (start us, length us, event | category | flops | bytes accessed | tf_op | source)
XLA Modules:
  0.0 66.4 jit_solution(10268643610475200764)
XLA Ops:
  0.6 63.3 %shard_map.77 = (bf16[1536,128]{1,0:T(8,128)(2,1)}, f32[4,128,128]{2,1,0:T(8,128)}) custom-call(bf16[64,1536]{1,0:T(8,128)(2,1)} %fac_hbm.1, bf16[64,2048]{1,0:T(8,128)(2,1)} %load_hbm.1, bf16[16,128]{1,0:T(8,128)(2,1)} %bitcast.7, bf16[16,128]{1,0:T(8,128)(2,1)} %bitcast.8, bf16[16,128]{1,0:T(8,128)(2,1)} %bitcast.9, s32[1,2048]{1,0:T(1,128)} %bitcast.6), custom_call_target="tpu_custom_call" | custom-call | tf_op jit(solution)/shard_map/pallas_call | solution.py:392
  63.9 0.0 copy-start
  63.9 1.8 %copy.10 = bf16[1536,128]{1,0:T(8,128)(2,1)} copy(bf16[1536,128]{1,0:T(8,128)(2,1)} %get-tuple-element.8) | data formatting | bytes 786432
  65.7 0.0 copy-done
  65.7 0.7 %copy.11 = f32[512,128]{1,0:T(8,128)} copy(f32[512,128]{1,0:T(8,128)S(1)} %bitcast.5) | data formatting | bytes 524288
Async XLA Ops:
  63.9 1.8 %copy-start = (f32[4,128,128]{2,1,0:T(8,128)S(1)}, f32[4,128,128]{2,1,0:T(8,128)}, u32[]{:S(2)}) copy-start(f32[4,128,128]{2,1,0:T(8,128)} %get-tuple-element.5) | copy-start | bytes 786436

commit v6 on v5

--- a/solution.py
+++ b/solution.py
@@ -11,10 +11,11 @@
 ROWS = 80
 SLOT = 128
 F = 64
-SIZES = (512, 512, 384, 128)
-STARTS = (0, 512, 1024, 1408)
+SIZES = (640, 512, 384)
+STARTS = (0, 640, 1152)
 CH = len(SIZES)
-FAR_SIDE = (0, 1, 1, 0)
+FAR_SIDE = (0, 1, 1)
+NQ, PER = 4, 8
 BF, F32 = jnp.bfloat16, jnp.float32
 NT = (((1,), (1,)), ((), ()))
 
@@ -27,17 +28,18 @@
 
 
 def kernel(fac_hbm, load_hbm, not_hbm, str_hbm, cur_hbm, id_hbm, exp_ref, mom_ref,
-           fac_ref, term_in, id_ref, desc, pack, trades, hot, ft, net, own, at0, at1, at2, at3,
+           fac_ref, term_in, id_ref, desc, pack, trades, hot, ft, net, own, at0, at1, at2,
            ring_in, acc, rsb, mid, rr, keep, turn, fa, fb, sin,
            s1, r1, s2, r2, sy, ry, sz, rz, srs, rrs, sa, ra, sb, rb):
     p = lax.axis_index("paths")
     c = lax.axis_index("cpty")
     z, y = c // NY, c % NY
-    at = (at0, at1, at2, at3)
+    at = (at0, at1, at2)
     paths = fac_ref.shape[1]
     count = id_ref.shape[1]
-    first = lax.rem(p - c + 32, 8)
-    targets = [first + 8 * i for i in range(4)]
+    quarter = 2 * (p // 2 % 2) + p % 2
+    first = lax.rem(quarter - c + NZ * NY, NQ)
+    targets = [first + NQ * i for i in range(PER)]
     x, core = p // 2, p % 2
     sign = 1 - 2 * core
     ahead, behind = lax.rem(z - sign + NZ, NZ), lax.rem(z + sign + NZ, NZ)
@@ -85,8 +87,8 @@
         base = base + jnp.sum(part, axis=1, keepdims=True)
         ranks.append(jnp.sum(part * before, axis=0, keepdims=True))
     rank = jnp.concatenate(ranks, axis=1).astype(jnp.int32)
-    mine = lax.rem(owner + c, 8) == p
-    code = jnp.where(mine, (owner // 8) * SLOT + rank, -1)
+    mine = lax.rem(owner + c, NQ) == quarter
+    code = jnp.where(mine, (owner // NQ) * SLOT + rank, -1)
     for copy in loads[1:5]:
         copy.wait()
     line = lax.broadcasted_iota(jnp.int32, (ROWS - F, count), 0)
@@ -96,20 +98,20 @@
         flat = jnp.concatenate([cells[k:k + 1, :] for k in range(count // CP)], axis=1)
         extra = jnp.where(line == i, flat, extra)
     desc[F:ROWS, :] = extra.astype(BF)
-    total = jnp.zeros((ROWS, 4 * SLOT), F32)
+    total = jnp.zeros((ROWS, PER * SLOT), F32)
     step = 512
     for b in range(count // step):
         cols = slice(b * step, (b + 1) * step)
-        chosen = (lax.broadcasted_iota(jnp.int32, (4 * SLOT, step), 0) == code[:, cols]).astype(F32).astype(BF)
+        chosen = (lax.broadcasted_iota(jnp.int32, (PER * SLOT, step), 0) == code[:, cols]).astype(F32).astype(BF)
         total = total + lax.dot_general(desc[:, cols], chosen, NT, preferred_element_type=F32)
-    for i in range(4):
+    for i in range(PER):
         pack[i] = total[:, i * SLOT:(i + 1) * SLOT].astype(BF)
 
-    pl.semaphore_wait(barrier, NP - 1 + 2 + NY - 1 + 4 - (lax.rem(2 * c, 8) == p).astype(jnp.int32))
-
-    place = c // 8
+    pl.semaphore_wait(barrier, NP - 1 + 2 + NY - 1 + PER - (lax.rem(2 * c, NQ) == quarter).astype(jnp.int32))
+
+    place = c // NQ
     for i, k in enumerate(targets):
-        copy = remote(pack.at[i], trades.at[p, place], s1.at[i], r1.at[place], p, k)
+        copy = remote(pack.at[i], trades.at[quarter, place], s1.at[i], r1.at[place], p, k)
 
         @pl.when(k != c)
         def _(copy=copy):
@@ -117,11 +119,11 @@
 
         @pl.when(k == c)
         def _(i=i):
-            trades[p, place] = pack[i]
+            trades[quarter, place] = pack[i]
     loads[5].wait()
     ft[...] = jnp.transpose(fac_ref[...].astype(F32)).astype(BF)
     for i, k in enumerate(targets):
-        arrive = remote(pack.at[i], trades.at[p, i], s1.at[i], r1.at[i], p, k)
+        arrive = remote(pack.at[i], trades.at[quarter, i], s1.at[i], r1.at[i], p, k)
 
         @pl.when(k != c)
         def _(arrive=arrive):
@@ -132,24 +134,19 @@
         copy.start()
         sends.append(copy)
 
-    x_ahead, x_back, x_far = lax.rem(x - sign + NX, NX), lax.rem(x + sign + NX, NX), lax.rem(x + 2, NX)
+    x_ahead = lax.rem(x - sign + NX, NX)
     partner = 2 * x + 1 - core
-    mates = [2 * i + core for i in (x, x_back, x_ahead, x_far)]
-    others = [2 * i + 1 - core for i in (x, x_ahead, x_back, x_far)]
-
-    def across(i):
-        return remote(trades.at[mates[i]], trades.at[mates[i]], s2.at[i], r2.at[i], partner, c)
-
-    def across_wait(i):
-        remote(trades.at[others[i]], trades.at[others[i]], s2.at[i], r2.at[i], partner, c).wait_recv()
-
-    def along(i):
-        src = mates[1] if i == 3 else p
-        dst = mates[1] if i == 2 else mates[2]
-        return remote(trades.at[src], trades.at[src], s2.at[NX + i], r2.at[NX + i], dst, c)
-
-    def along_wait(i):
-        remote(trades.at[mates[i]], trades.at[mates[i]], s2.at[NX + i], r2.at[NX + i], partner, c).wait_recv()
+    own_q, mate_q = quarter, quarter + 1 - 2 * core
+    beside_q, last_q = lax.rem(own_q + 2, NQ), lax.rem(mate_q + 2, NQ)
+
+    def give(i):
+        part = beside_q if i == 2 else own_q
+        to = 2 * x_ahead + core if i == 1 else partner
+        return remote(trades.at[part], trades.at[part], s2.at[i], r2.at[i], to, c)
+
+    def given(i):
+        part = (mate_q, beside_q, last_q)[i]
+        remote(trades.at[part], trades.at[part], s2.at[i], r2.at[i], partner, c).wait_recv()
 
     def span(j):
         return slice(STARTS[j], STARTS[j] + SIZES[j])
@@ -157,16 +154,15 @@
     def cut(j):
         return pl.ds(STARTS[j], SIZES[j])
 
-    def tile_of(pp):
-        t = trades[pp]
-        return jnp.concatenate([t[i] for i in range(4)], axis=1)
-
-    def price(j, pp):
-        full = tile_of(pp)
+    def tile_of(g, h):
+        return jnp.concatenate([trades[g, 4 * h + i] for i in range(4)], axis=1)
+
+    def price(j, g, h):
+        full = tile_of(g, h)
         terms = full[F:ROWS, :].astype(F32)
         lin = jnp.dot(ft[span(j), :], full[0:F, :], preferred_element_type=F32)
         value = terms[0:1, :] * (lin + terms[2:3, :] * jnp.tanh(lin - terms[1:2, :]))
-        return lax.dot_general(value.astype(BF), hot[pp], NT, preferred_element_type=F32)
+        return lax.dot_general(value.astype(BF), hot[2 * g + h], NT, preferred_element_type=F32)
 
     def ring(s, j):
         src = own.at[cut(j)] if s == 0 else ring_in.at[s - 1, cut(j)]
@@ -251,46 +247,33 @@
         def _():
             fa[core, y] = turn[d]
 
-    for t in range(CH + FAR + 1):
+    for t in range(CH + FAR):
         if t < CH:
             j = t
             here = net.at[0:SIZES[j], :]
 
-            def take(*group):
-                for pp in group:
-                    t4 = trades[pp]
-                    label = jnp.concatenate([t4[i][F:ROWS, :] for i in range(4)], axis=1).astype(F32)[3:4, :]
-                    hot[pp] = (lax.broadcasted_iota(jnp.int32, (CP, 4 * SLOT), 0).astype(F32) == label).astype(F32).astype(BF)
-                here[...] += sum(price(0, pp) for pp in group)
+            def take(g):
+                for h in range(2):
+                    label = tile_of(g, h)[F:ROWS, :].astype(F32)[3:4, :]
+                    hot[2 * g + h] = (lax.broadcasted_iota(jnp.int32, (CP, 4 * SLOT), 0).astype(F32) == label).astype(F32).astype(BF)
+                return price(0, g, 0) + price(0, g, 1)
 
             if j == 0:
-                go(along(1))
-                go(along(2))
-                go(across(0))
-                here[...] = jnp.zeros_like(here)
-                across_wait(0)
-                take(p, others[0])
-                along_wait(1)
-                go(along(3))
-                go(across(1))
-                along_wait(2)
-                go(across(2))
-                take(mates[1], mates[2])
-                across_wait(1)
-                across_wait(2)
-                take(others[1], others[2])
-                along_wait(3)
-                go(across(3))
-                across_wait(3)
-                take(mates[3], others[3])
+                for i in range(2):
+                    go(give(i))
+                here[...] = take(own_q)
+                given(0)
+                here[...] += take(mate_q)
+                given(1)
+                go(give(2))
+                here[...] += take(beside_q)
+                given(2)
+                here[...] += take(last_q)
             else:
                 here[...] = jnp.zeros_like(here)
-
-                def body(r, _):
-                    here[...] += price(j, r)
-                    return 0
-
-                lax.fori_loop(0, NP, body, 0, unroll=NP)
+                for g in range(NQ):
+                    for h in range(2):
+                        here[...] += price(j, g, h)
             block_f = jnp.maximum(here[...], 0.0)
             block_b = block_f.astype(BF)
             own[span(j), :] = block_b
@@ -300,7 +283,7 @@
             go(side(j, 0))
             go(side(j, 1))
         for s in range(1, FAR):
-            j = t - 1 - s
+            j = t - s
             if 0 <= j < CH:
                 ring(s - 1, j).wait_recv()
                 if s < FAR - 1:
@@ -311,19 +294,16 @@
                     @pl.when(far_ahead == FAR_SIDE[j])
                     def _(copy=copy):
                         copy.start()
-        for j in {2: (0,), 3: (1,), 4: (2, 3)}.get(t, ()):
+        for j in {2: (0,), 3: (1, 2)}.get(t, ()):
             side_wait(j, 0)
             go(side(j, 2))
             side_wait(j, 1)
         j = t - 3
         if 0 <= j < CH - 1:
             side_wait(j, 2)
-            for d in (0, 1, 2):
+            for d in (0, 1, 2, 3):
                 dots(d, j)
-        j = t - 4
-        if 0 <= j < CH:
-            dots(3, j)
-        j = t - 1 - FAR
+        j = t - FAR
         if 0 <= j < CH:
             @pl.when(far_here == FAR_SIDE[j])
             def _(j=j):
@@ -331,13 +311,11 @@
                 dots(FAR, j, j < 2)
         if t == CH + 1:
             side_wait(CH - 1, 2)
-            for d in (0, 1):
+            for d in (0, 1, 2):
                 dots(d, CH - 1)
                 ship(d)
         if t == CH + 2:
-            dots(2, CH - 1)
-            ship(2)
-        if t == CH + 3:
+            dots(3, CH - 1)
             ship(3)
             pass_on(0)
             pass_on(1)
@@ -366,7 +344,7 @@
                 mom_ref[i] += fb[k, i].astype(F32)
 
     for i, k in enumerate(targets):
-        copy = remote(pack.at[i], trades.at[p, place], s1.at[i], r1.at[place], p, k)
+        copy = remote(pack.at[i], trades.at[quarter, place], s1.at[i], r1.at[place], p, k)
 
         @pl.when(k != c)
         def _(copy=copy):
@@ -399,8 +377,8 @@
             pltpu.VMEM((3, count // CP, CP), BF),
             pltpu.VMEM((1, count), jnp.int32),
             pltpu.VMEM((ROWS, count), BF),
-            pltpu.VMEM((4, ROWS, SLOT), BF),
-            pltpu.VMEM((NP, 4, ROWS, SLOT), BF),
+            pltpu.VMEM((PER, ROWS, SLOT), BF),
+            pltpu.VMEM((NQ, PER, ROWS, SLOT), BF),
             pltpu.VMEM((NP, CP, 4 * SLOT), BF),
             pltpu.VMEM((paths, F), BF),
             pltpu.VMEM((max(SIZES), CP), F32),
@@ -415,7 +393,7 @@
             pltpu.VMEM((FAR + 1, CP, CP), BF),
             pltpu.VMEM((2, NY, CP, CP), BF),
             pltpu.VMEM((2, NX, CP, CP), BF),
-            dma((6,)), dma((4,)), dma((4,)), dma((NP,)), dma((NP,)),
+            dma((6,)), dma((PER,)), dma((PER,)), dma((3,)), dma((3,)),
             dma((CH, 3)), dma((CH, 3)), dma((FAR, CH)), dma((FAR, CH)),
             dma((FAR + 1, 3)), dma((FAR + 1, 3)),
             dma((FAR + 1,)), dma((2, NY)), dma((FAR + 1,)), dma((2, NX)),

time: 66.5 us -> 63.9 us (0.961)
  Pallas kernels: 63.3 us -> 60.5 us
    pallas_call x1, Pallas kernels: 63.3 us -> 60.5 us  [on_device(): pl.pallas_call(kernel, out_shape=(jax.ShapeDtypeStruct((paths, CP), BF),...]
where the time goes in v6:
time: 63.9 us; the launch traced here: 63.7 us
  Pallas kernels  60.5 us (95%)
  local copies, waits for them, and re-layouts  2.52 us (4%)
  between operations  0.65 us (1%)
    pallas_call x1, Pallas kernels, on_device(): pl.pallas_call(kernel, out_shape=(jax.ShapeDtypeStruct((paths, CP), BF),...  60.5 us
    unnamed x4, local copies, waits for them, and re-layouts  2.52 us

profile of v6, /device:TPU:4, one launch (start us, length us, event | category | flops | bytes accessed | tf_op | source)
XLA Modules:
  0.0 63.7 jit_solution(16551461829754021147)
XLA Ops:
  0.6 60.5 %shard_map.77 = (bf16[1536,128]{1,0:T(8,128)(2,1)}, f32[4,128,128]{2,1,0:T(8,128)}) custom-call(bf16[64,1536]{1,0:T(8,128)(2,1)} %fac_hbm.1, bf16[64,2048]{1,0:T(8,128)(2,1)} %load_hbm.1, bf16[16,128]{1,0:T(8,128)(2,1)} %bitcast.7, bf16[16,128]{1,0:T(8,128)(2,1)} %bitcast.8, bf16[16,128]{1,0:T(8,128)(2,1)} %bitcast.9, s32[1,2048]{1,0:T(1,128)} %bitcast.6), custom_call_target="tpu_custom_call" | custom-call | tf_op jit(solution)/shard_map/pallas_call | solution.py:370
  61.1 0.0 copy-start
  61.1 1.8 %copy.10 = bf16[1536,128]{1,0:T(8,128)(2,1)} copy(bf16[1536,128]{1,0:T(8,128)(2,1)} %get-tuple-element.8) | data formatting | bytes 786432
  62.9 0.0 copy-done
  63.0 0.7 %copy.11 = f32[512,128]{1,0:T(8,128)} copy(f32[512,128]{1,0:T(8,128)S(1)} %bitcast.5) | data formatting | bytes 524288
Async XLA Ops:
  61.1 1.8 %copy-start = (f32[4,128,128]{2,1,0:T(8,128)S(1)}, f32[4,128,128]{2,1,0:T(8,128)}, u32[]{:S(2)}) copy-start(f32[4,128,128]{2,1,0:T(8,128)} %get-tuple-element.5) | copy-start | bytes 786436

commit v7 on v6

--- a/solution.py
+++ b/solution.py
@@ -247,80 +247,95 @@
         def _():
             fa[core, y] = turn[d]
 
-    for t in range(CH + FAR):
-        if t < CH:
-            j = t
-            here = net.at[0:SIZES[j], :]
-
-            def take(g):
+    def relay(s, j):
+        ring(s - 1, j).wait_recv()
+        if s < FAR - 1:
+            go(ring(s, j))
+        else:
+            copy = ring(s, j)
+
+            @pl.when(far_ahead == FAR_SIDE[j])
+            def _():
+                copy.start()
+
+    def side_relay(j):
+        side_wait(j, 0)
+        go(side(j, 2))
+        side_wait(j, 1)
+
+    def far(j):
+        @pl.when(far_here == FAR_SIDE[j])
+        def _():
+            ring(FAR - 1, j).wait_recv()
+            dots(FAR, j, j < 2)
+
+    for j in range(CH):
+        here = net.at[0:SIZES[j], :]
+
+        def take(g):
+            for h in range(2):
+                label = tile_of(g, h)[F:ROWS, :].astype(F32)[3:4, :]
+                hot[2 * g + h] = (lax.broadcasted_iota(jnp.int32, (CP, 4 * SLOT), 0).astype(F32) == label).astype(F32).astype(BF)
+            return price(0, g, 0) + price(0, g, 1)
+
+        if j == 0:
+            for i in range(2):
+                go(give(i))
+            here[...] = take(own_q)
+            given(0)
+            here[...] += take(mate_q)
+            given(1)
+            go(give(2))
+            here[...] += take(beside_q)
+            given(2)
+            here[...] += take(last_q)
+        else:
+            here[...] = jnp.zeros_like(here)
+            for g in range(NQ):
                 for h in range(2):
-                    label = tile_of(g, h)[F:ROWS, :].astype(F32)[3:4, :]
-                    hot[2 * g + h] = (lax.broadcasted_iota(jnp.int32, (CP, 4 * SLOT), 0).astype(F32) == label).astype(F32).astype(BF)
-                return price(0, g, 0) + price(0, g, 1)
-
-            if j == 0:
-                for i in range(2):
-                    go(give(i))
-                here[...] = take(own_q)
-                given(0)
-                here[...] += take(mate_q)
-                given(1)
-                go(give(2))
-                here[...] += take(beside_q)
-                given(2)
-                here[...] += take(last_q)
-            else:
-                here[...] = jnp.zeros_like(here)
-                for g in range(NQ):
-                    for h in range(2):
-                        here[...] += price(j, g, h)
-            block_f = jnp.maximum(here[...], 0.0)
-            block_b = block_f.astype(BF)
-            own[span(j), :] = block_b
-            exp_ref[span(j), :] = block_b
-            at[j][y] = jnp.transpose(block_f).astype(BF)
-            go(ring(0, j))
-            go(side(j, 0))
-            go(side(j, 1))
-        for s in range(1, FAR):
-            j = t - s
-            if 0 <= j < CH:
-                ring(s - 1, j).wait_recv()
-                if s < FAR - 1:
-                    go(ring(s, j))
-                else:
-                    copy = ring(s, j)
-
-                    @pl.when(far_ahead == FAR_SIDE[j])
-                    def _(copy=copy):
-                        copy.start()
-        for j in {2: (0,), 3: (1, 2)}.get(t, ()):
-            side_wait(j, 0)
-            go(side(j, 2))
-            side_wait(j, 1)
-        j = t - 3
-        if 0 <= j < CH - 1:
-            side_wait(j, 2)
-            for d in (0, 1, 2, 3):
-                dots(d, j)
-        j = t - FAR
-        if 0 <= j < CH:
-            @pl.when(far_here == FAR_SIDE[j])
-            def _(j=j):
-                ring(FAR - 1, j).wait_recv()
-                dots(FAR, j, j < 2)
-        if t == CH + 1:
-            side_wait(CH - 1, 2)
-            for d in (0, 1, 2):
-                dots(d, CH - 1)
-                ship(d)
-        if t == CH + 2:
-            dots(3, CH - 1)
-            ship(3)
-            pass_on(0)
-            pass_on(1)
-            pass_on(2)
+                    here[...] += price(j, g, h)
+        block_f = jnp.maximum(here[...], 0.0)
+        block_b = block_f.astype(BF)
+        own[span(j), :] = block_b
+        exp_ref[span(j), :] = block_b
+        at[j][y] = jnp.transpose(block_f).astype(BF)
+        go(ring(0, j))
+        go(side(j, 0))
+        go(side(j, 1))
+        if j == 1:
+            relay(1, 0)
+    relay(1, 1)
+    side_relay(0)
+    relay(2, 0)
+    side_relay(1)
+    relay(1, 2)
+    relay(2, 1)
+    side_relay(2)
+    side_wait(0, 2)
+    for d in (0, 1, 2):
+        dots(d, 0)
+    relay(3, 0)
+    dots(3, 0)
+    relay(2, 2)
+    side_wait(1, 2)
+    for d in (0, 1, 2):
+        dots(d, 1)
+    relay(3, 1)
+    dots(3, 1)
+    side_wait(2, 2)
+    for d in (0, 1, 2):
+        dots(d, 2)
+        ship(d)
+    relay(3, 2)
+    dots(3, 2)
+    ship(3)
+    far(0)
+    far(1)
+    pass_on(0)
+    pass_on(1)
+    far(2)
     ship(FAR)
+    pass_on(2)
     for d in range(FAR + 1):
         collect(d)
 

time: 63.9 us -> 61.9 us (0.969)
  Pallas kernels: 60.5 us -> 58.1 us
    pallas_call x1, Pallas kernels: 60.5 us -> 58.1 us  [on_device(): pl.pallas_call(kernel, out_shape=(jax.ShapeDtypeStruct((paths, CP), BF),...]
where the time goes in v7:
time: 61.9 us; the launch traced here: 61.3 us
  Pallas kernels  58.1 us (94%)
  local copies, waits for them, and re-layouts  2.52 us (4%)
  between operations  0.65 us (1%)
    pallas_call x1, Pallas kernels, on_device(): pl.pallas_call(kernel, out_shape=(jax.ShapeDtypeStruct((paths, CP), BF),...  58.1 us
    unnamed x4, local copies, waits for them, and re-layouts  2.52 us

profile of v7, /device:TPU:4, one launch (start us, length us, event | category | flops | bytes accessed | tf_op | source)
XLA Modules:
  0.0 61.3 jit_solution(14346257982916343811)
XLA Ops:
  0.6 58.1 %shard_map.77 = (bf16[1536,128]{1,0:T(8,128)(2,1)}, f32[4,128,128]{2,1,0:T(8,128)}) custom-call(bf16[64,1536]{1,0:T(8,128)(2,1)} %fac_hbm.1, bf16[64,2048]{1,0:T(8,128)(2,1)} %load_hbm.1, bf16[16,128]{1,0:T(8,128)(2,1)} %bitcast.7, bf16[16,128]{1,0:T(8,128)(2,1)} %bitcast.8, bf16[16,128]{1,0:T(8,128)(2,1)} %bitcast.9, s32[1,2048]{1,0:T(1,128)} %bitcast.6), custom_call_target="tpu_custom_call" | custom-call | tf_op jit(solution)/shard_map/pallas_call | solution.py:385
  58.8 0.0 copy-start
  58.8 1.8 %copy.10 = bf16[1536,128]{1,0:T(8,128)(2,1)} copy(bf16[1536,128]{1,0:T(8,128)(2,1)} %get-tuple-element.8) | data formatting | bytes 786432
  60.6 0.0 copy-done
  60.6 0.7 %copy.11 = f32[512,128]{1,0:T(8,128)} copy(f32[512,128]{1,0:T(8,128)S(1)} %bitcast.5) | data formatting | bytes 524288
Async XLA Ops:
  58.8 1.8 %copy-start = (f32[4,128,128]{2,1,0:T(8,128)S(1)}, f32[4,128,128]{2,1,0:T(8,128)}, u32[]{:S(2)}) copy-start(f32[4,128,128]{2,1,0:T(8,128)} %get-tuple-element.5) | copy-start | bytes 786436

commit v8 on v7

--- a/solution.py
+++ b/solution.py
@@ -30,7 +30,7 @@
 def kernel(fac_hbm, load_hbm, not_hbm, str_hbm, cur_hbm, id_hbm, exp_ref, mom_ref,
            fac_ref, term_in, id_ref, desc, pack, trades, hot, ft, net, own, at0, at1, at2,
            ring_in, acc, rsb, mid, rr, keep, turn, fa, fb, sin,
-           s1, r1, s2, r2, sy, ry, sz, rz, srs, rrs, sa, ra, sb, rb):
+           sout, s1, r1, s2, r2, sy, ry, sz, rz, srs, rrs, sa, ra, sb, rb):
     p = lax.axis_index("paths")
     c = lax.axis_index("cpty")
     z, y = c // NY, c % NY
@@ -110,16 +110,19 @@
     pl.semaphore_wait(barrier, NP - 1 + 2 + NY - 1 + PER - (lax.rem(2 * c, NQ) == quarter).astype(jnp.int32))
 
     place = c // NQ
-    for i, k in enumerate(targets):
-        copy = remote(pack.at[i], trades.at[quarter, place], s1.at[i], r1.at[place], p, k)
-
-        @pl.when(k != c)
-        def _(copy=copy):
+    for offset in (4, 3, 5, 2, 6, 1, 7, 0):
+        i = lax.rem(z + offset, PER)
+        copy = remote(pack.at[i], trades.at[quarter, place], s1.at[i], r1.at[place], p, first + NQ * i)
+        if offset:
             copy.start()
-
-        @pl.when(k == c)
-        def _(i=i):
-            trades[quarter, place] = pack[i]
+        else:
+            @pl.when(first != y)
+            def _(copy=copy):
+                copy.start()
+
+            @pl.when(first == y)
+            def _(i=i):
+                trades[quarter, place] = pack[i]
     loads[5].wait()
     ft[...] = jnp.transpose(fac_ref[...].astype(F32)).astype(BF)
     for i, k in enumerate(targets):
@@ -246,6 +249,9 @@
         @pl.when(turned_home(d))
         def _():
             fa[core, y] = turn[d]
+
+    def out(j):
+        return pltpu.make_async_copy(own.at[cut(j)], exp_ref.at[cut(j)], sout.at[j])
 
     def relay(s, j):
         ring(s - 1, j).wait_recv()
@@ -297,9 +303,9 @@
         block_f = jnp.maximum(here[...], 0.0)
         block_b = block_f.astype(BF)
         own[span(j), :] = block_b
-        exp_ref[span(j), :] = block_b
         at[j][y] = jnp.transpose(block_f).astype(BF)
         go(ring(0, j))
+        out(j).start()
         go(side(j, 0))
         go(side(j, 1))
         if j == 1:
@@ -314,28 +320,27 @@
     side_wait(0, 2)
     for d in (0, 1, 2):
         dots(d, 0)
+    relay(2, 2)
     relay(3, 0)
     dots(3, 0)
-    relay(2, 2)
     side_wait(1, 2)
     for d in (0, 1, 2):
         dots(d, 1)
     relay(3, 1)
-    dots(3, 1)
     side_wait(2, 2)
     for d in (0, 1, 2):
         dots(d, 2)
         ship(d)
     relay(3, 2)
-    dots(3, 2)
+    for j in (1, 2):
+        dots(3, j)
     ship(3)
     far(0)
     far(1)
-    pass_on(0)
-    pass_on(1)
+    for d in (0, 1, 2):
+        pass_on(d)
     far(2)
     ship(FAR)
-    pass_on(2)
     for d in range(FAR + 1):
         collect(d)
 
@@ -358,6 +363,8 @@
                 remote(turn.at[0], fb.at[k, i], sb.at[0], rb.at[k, i], 2 * i + k, p * NY + y).wait_recv()
                 mom_ref[i] += fb[k, i].astype(F32)
 
+    for j in range(CH):
+        out(j).wait()
     for i, k in enumerate(targets):
         copy = remote(pack.at[i], trades.at[quarter, place], s1.at[i], r1.at[place], p, k)
 
@@ -376,6 +383,24 @@
         @pl.when(jnp.logical_not(turned_home(d)))
         def _(d=d):
             turned(d).wait_send()
+
+
+def hand_out(exp_in, mom_in, exp_out, mom_out, exp_buf, mom_buf, sin, sout):
+    steps = []
+    for a, (src, buf, dst) in enumerate(((exp_in, exp_buf, exp_out), (mom_in, mom_buf, mom_out))):
+        rows = src.shape[0] // 4
+        for i in range(4):
+            part = pl.ds(i * rows, rows)
+            steps.append((
+                pltpu.make_async_copy(src.at[part], buf.at[part], sin.at[a, i]),
+                pltpu.make_async_copy(buf.at[part], dst.at[part], sout.at[a, i])))
+    for get, _ in steps:
+        get.start()
+    for get, put in steps:
+        get.wait()
+        put.start()
+    for _, put in steps:
+        put.wait()
 
 
 def on_device(factors, loadings, notional, strike, curvature, trade_cpty):
@@ -386,7 +411,7 @@
         kernel,
         out_shape=(jax.ShapeDtypeStruct((paths, CP), BF), jax.ShapeDtypeStruct((NY, CP, CP), F32)),
         in_specs=[pl.BlockSpec(memory_space=pl.ANY)] * 6,
-        out_specs=(vmem, vmem),
+        out_specs=(pl.BlockSpec(memory_space=pl.ANY), vmem),
         scratch_shapes=[
             pltpu.VMEM((F, paths), BF),
             pltpu.VMEM((3, count // CP, CP), BF),
@@ -408,7 +433,7 @@
             pltpu.VMEM((FAR + 1, CP, CP), BF),
             pltpu.VMEM((2, NY, CP, CP), BF),
             pltpu.VMEM((2, NX, CP, CP), BF),
-            dma((6,)), dma((PER,)), dma((PER,)), dma((3,)), dma((3,)),
+            dma((6,)), dma((CH,)), dma((PER,)), dma((PER,)), dma((3,)), dma((3,)),
             dma((CH, 3)), dma((CH, 3)), dma((FAR, CH)), dma((FAR, CH)),
             dma((FAR + 1, 3)), dma((FAR + 1, 3)),
             dma((FAR + 1,)), dma((2, NY)), dma((FAR + 1,)), dma((2, NX)),
@@ -417,6 +442,16 @@
             collective_id=0, has_side_effects=True, vmem_limit_bytes=67043328),
     )(factors, loadings, *[a.reshape(count // CP, CP) for a in (notional, strike, curvature)],
       trade_cpty[None, :])
+    shapes = [(exposure.shape, BF), (moment.shape, F32)]
+    anywhere = pl.BlockSpec(memory_space=pl.ANY)
+    exposure, moment = pl.pallas_call(
+        hand_out,
+        out_shape=tuple(jax.ShapeDtypeStruct(*s) for s in shapes),
+        in_specs=[anywhere] * 2,
+        out_specs=(anywhere,) * 2,
+        scratch_shapes=[*[pltpu.VMEM(*s) for s in shapes], dma((2, 4)), dma((2, 4))],
+        compiler_params=pltpu.CompilerParams(vmem_limit_bytes=67043328),
+    )(exposure, moment)
     return exposure, moment.reshape(NY * CP, CP)
 
 

time: 61.9 us -> 60.7 us (0.981)
  local copies, waits for them, and re-layouts: 2.52 us -> 0 us
  Pallas kernels: 58.1 us -> 59.9 us
    unnamed x4 -> x0, local copies, waits for them, and re-layouts: 2.52 us -> none
    pallas_call x0 -> x1, Pallas kernels: none -> 1.9 us  [on_device(): pl.pallas_call(hand_out, out_shape=tuple((jax.ShapeDtypeStruct(*s) for s...]
where the time goes in v8:
time: 60.7 us; the launch traced here: 60.5 us
  Pallas kernels  59.9 us (99%)
  between operations  0.64 us (1%)
    pallas_call x1, Pallas kernels, on_device(): pl.pallas_call(kernel, out_shape=(jax.ShapeDtypeStruct((paths, CP), BF),...  58 us
    pallas_call x1, Pallas kernels, on_device(): pl.pallas_call(hand_out, out_shape=tuple((jax.ShapeDtypeStruct(*s) for s...  1.9 us

profile of v8, /device:TPU:4, one launch (start us, length us, event | category | flops | bytes accessed | tf_op | source)
XLA Modules:
  0.0 60.5 jit_solution(12868875398885668129)
XLA Ops:
  0.6 58.0 %shard_map.77 = (bf16[1536,128]{1,0:T(8,128)(2,1)}, f32[4,128,128]{2,1,0:T(8,128)}) custom-call(bf16[64,1536]{1,0:T(8,128)(2,1)} %fac_hbm.1, bf16[64,2048]{1,0:T(8,128)(2,1)} %load_hbm.1, bf16[16,128]{1,0:T(8,128)(2,1)} %bitcast.6, bf16[16,128]{1,0:T(8,128)(2,1)} %bitcast.7, bf16[16,128]{1,0:T(8,128)(2,1)} %bitcast.8, s32[1,2048]{1,0:T(1,128)} %bitcast.5), custom_call_target="tpu_custom_call" | custom-call | tf_op jit(solution)/shard_map/pallas_call | solution.py:410
  58.6 1.9 %shard_map.78 = (bf16[1536,128]{1,0:T(8,128)(2,1)}, f32[4,128,128]{2,1,0:T(8,128)}) custom-call(bf16[1536,128]{1,0:T(8,128)(2,1)} %get-tuple-element.6.exp_in, f32[4,128,128]{2,1,0:T(8,128)} %get-tuple-element.7.mom_in), custom_call_target="tpu_custom_call" | custom-call | tf_op jit(solution)/shard_map/pallas_call | solution.py:447

commit v9 on v8

--- a/solution.py
+++ b/solution.py
@@ -14,7 +14,6 @@
 SIZES = (640, 512, 384)
 STARTS = (0, 640, 1152)
 CH = len(SIZES)
-FAR_SIDE = (0, 1, 1)
 NQ, PER = 4, 8
 BF, F32 = jnp.bfloat16, jnp.float32
 NT = (((1,), (1,)), ((), ()))
@@ -44,7 +43,6 @@
     sign = 1 - 2 * core
     ahead, behind = lax.rem(z - sign + NZ, NZ), lax.rem(z + sign + NZ, NZ)
     y_ahead, y_back = lax.rem(y - sign + NY, NY), lax.rem(y + sign + NY, NY)
-    far_here, far_ahead = z // FAR, ahead // FAR
 
     barrier = pltpu.get_barrier_semaphore()
 
@@ -142,14 +140,17 @@
     own_q, mate_q = quarter, quarter + 1 - 2 * core
     beside_q, last_q = lax.rem(own_q + 2, NQ), lax.rem(mate_q + 2, NQ)
 
-    def give(i):
+    def half(part, h):
+        return trades.at[part, pl.ds(4 * h, 4)]
+
+    def give(i, h):
         part = beside_q if i == 2 else own_q
         to = 2 * x_ahead + core if i == 1 else partner
-        return remote(trades.at[part], trades.at[part], s2.at[i], r2.at[i], to, c)
-
-    def given(i):
+        return remote(half(part, h), half(part, h), s2.at[i, h], r2.at[i, h], to, c)
+
+    def given(i, h):
         part = (mate_q, beside_q, last_q)[i]
-        remote(trades.at[part], trades.at[part], s2.at[i], r2.at[i], partner, c).wait_recv()
+        remote(half(part, h), half(part, h), s2.at[i, h], r2.at[i, h], partner, c).wait_recv()
 
     def span(j):
         return slice(STARTS[j], STARTS[j] + SIZES[j])
@@ -189,9 +190,9 @@
     def left(j):
         return at[j][...].reshape(NY * CP, SIZES[j])
 
-    def dots(d, j, start=None):
+    def dots(d, j):
         right = own[span(j), :] if d == 0 else ring_in[d - 1, span(j), :]
-        add(d, j, jnp.dot(left(j), right, preferred_element_type=F32), j == 0 if start is None else start)
+        add(d, j, jnp.dot(left(j), right, preferred_element_type=F32), j == 0)
 
     def cell(d):
         return lax.rem(z + sign * d + NZ, NZ)
@@ -237,7 +238,7 @@
             reduce(d, i).wait_recv()
             whole = whole + rr[d, i].astype(F32)
         whole = whole * (1.0 / (paths * NP))
-        if d > 0:
+        if 0 < d < FAR:
             keep[d] = whole.astype(BF)
             go(direct(d))
         turn[d] = jnp.transpose(whole).astype(BF)
@@ -255,14 +256,7 @@
 
     def relay(s, j):
         ring(s - 1, j).wait_recv()
-        if s < FAR - 1:
-            go(ring(s, j))
-        else:
-            copy = ring(s, j)
-
-            @pl.when(far_ahead == FAR_SIDE[j])
-            def _():
-                copy.start()
+        go(ring(s, j))
 
     def side_relay(j):
         side_wait(j, 0)
@@ -270,31 +264,34 @@
         side_wait(j, 1)
 
     def far(j):
-        @pl.when(far_here == FAR_SIDE[j])
-        def _():
-            ring(FAR - 1, j).wait_recv()
-            dots(FAR, j, j < 2)
+        ring(FAR - 1, j).wait_recv()
+        dots(FAR, j)
 
     for j in range(CH):
         here = net.at[0:SIZES[j], :]
 
-        def take(g):
-            for h in range(2):
+        def take(g, halves=(0, 1)):
+            for h in halves:
                 label = tile_of(g, h)[F:ROWS, :].astype(F32)[3:4, :]
                 hot[2 * g + h] = (lax.broadcasted_iota(jnp.int32, (CP, 4 * SLOT), 0).astype(F32) == label).astype(F32).astype(BF)
-            return price(0, g, 0) + price(0, g, 1)
+            return sum(price(0, g, h) for h in halves)
 
         if j == 0:
-            for i in range(2):
-                go(give(i))
+            for i in (1, 0):
+                for h in range(2):
+                    go(give(i, h))
             here[...] = take(own_q)
-            given(0)
+            for h in range(2):
+                given(0, h)
             here[...] += take(mate_q)
-            given(1)
-            go(give(2))
+            for h in range(2):
+                given(1, h)
+                go(give(2, h))
             here[...] += take(beside_q)
-            given(2)
-            here[...] += take(last_q)
+            given(2, 0)
+            here[...] += take(last_q, (0,))
+            given(2, 1)
+            here[...] += take(last_q, (1,))
         else:
             here[...] = jnp.zeros_like(here)
             for g in range(NQ):
@@ -341,14 +338,14 @@
         pass_on(d)
     far(2)
     ship(FAR)
-    for d in range(FAR + 1):
+    for d in (3, 0, 1, 2, FAR):
         collect(d)
 
     delta = lax.rem(p - z + NZ, NZ)
     mom_ref[...] = jnp.zeros_like(mom_ref)
     for k in range(2):
         near = (delta <= FAR) if k == 0 else ((delta >= FAR) | (delta == 0))
-        away = ((delta >= FAR) if k == 0 else ((delta <= FAR) & (delta > 0)))
+        away = (delta > FAR) if k == 0 else ((delta < FAR) & (delta > 0))
         for i in range(NY):
             @pl.when(near & jnp.logical_not((core == k) & (i == y) & (x == y)))
             def _(k=k, i=i):
@@ -373,12 +370,6 @@
             copy.wait_send()
     for copy in sends:
         copy.wait_send()
-    for j in range(CH):
-        copy = ring(FAR - 1, j)
-
-        @pl.when(far_ahead == FAR_SIDE[j])
-        def _(copy=copy):
-            copy.wait_send()
     for d in range(FAR + 1):
         @pl.when(jnp.logical_not(turned_home(d)))
         def _(d=d):
@@ -433,7 +424,7 @@
             pltpu.VMEM((FAR + 1, CP, CP), BF),
             pltpu.VMEM((2, NY, CP, CP), BF),
             pltpu.VMEM((2, NX, CP, CP), BF),
-            dma((6,)), dma((CH,)), dma((PER,)), dma((PER,)), dma((3,)), dma((3,)),
+            dma((6,)), dma((CH,)), dma((PER,)), dma((PER,)), dma((3, 2)), dma((3, 2)),
             dma((CH, 3)), dma((CH, 3)), dma((FAR, CH)), dma((FAR, CH)),
             dma((FAR + 1, 3)), dma((FAR + 1, 3)),
             dma((FAR + 1,)), dma((2, NY)), dma((FAR + 1,)), dma((2, NX)),

time: 60.7 us -> 60 us (0.988)
  Pallas kernels: 59.9 us -> 59.2 us
    pallas_call x1, Pallas kernels: 58 us -> 57.3 us  [on_device(): pl.pallas_call(kernel, out_shape=(jax.ShapeDtypeStruct((paths, CP), BF),...]
where the time goes in v9:
time: 60 us; the launch traced here: 59.8 us
  Pallas kernels  59.2 us (99%)
  between operations  0.64 us (1%)
    pallas_call x1, Pallas kernels, on_device(): pl.pallas_call(kernel, out_shape=(jax.ShapeDtypeStruct((paths, CP), BF),...  57.3 us
    pallas_call x1, Pallas kernels, on_device(): pl.pallas_call(hand_out, out_shape=tuple((jax.ShapeDtypeStruct(*s) for s...  1.9 us

profile of v9, /device:TPU:4, one launch (start us, length us, event | category | flops | bytes accessed | tf_op | source)
XLA Modules:
  0.0 59.8 jit_solution(7356894863767600200)
XLA Ops:
  0.6 57.3 %shard_map.77 = (bf16[1536,128]{1,0:T(8,128)(2,1)}, f32[4,128,128]{2,1,0:T(8,128)}) custom-call(bf16[64,1536]{1,0:T(8,128)(2,1)} %fac_hbm.1, bf16[64,2048]{1,0:T(8,128)(2,1)} %load_hbm.1, bf16[16,128]{1,0:T(8,128)(2,1)} %bitcast.6, bf16[16,128]{1,0:T(8,128)(2,1)} %bitcast.7, bf16[16,128]{1,0:T(8,128)(2,1)} %bitcast.8, s32[1,2048]{1,0:T(1,128)} %bitcast.5), custom_call_target="tpu_custom_call" | custom-call | tf_op jit(solution)/shard_map/pallas_call | solution.py:401
  57.9 1.9 %shard_map.78 = (bf16[1536,128]{1,0:T(8,128)(2,1)}, f32[4,128,128]{2,1,0:T(8,128)}) custom-call(bf16[1536,128]{1,0:T(8,128)(2,1)} %get-tuple-element.6.exp_in, f32[4,128,128]{2,1,0:T(8,128)} %get-tuple-element.7.mom_in), custom_call_target="tpu_custom_call" | custom-call | tf_op jit(solution)/shard_map/pallas_call | solution.py:438

commit v10 on v9

--- a/solution.py
+++ b/solution.py
@@ -44,6 +44,15 @@
     ahead, behind = lax.rem(z - sign + NZ, NZ), lax.rem(z + sign + NZ, NZ)
     y_ahead, y_back = lax.rem(y - sign + NY, NY), lax.rem(y + sign + NY, NY)
 
+    loads = [
+        pltpu.make_async_copy(src, dst, sin.at[i])
+        for i, (src, dst) in enumerate((
+            (id_hbm, id_ref), (not_hbm, term_in.at[0]), (str_hbm, term_in.at[1]),
+            (cur_hbm, term_in.at[2]), (load_hbm, desc.at[0:F, :]), (fac_hbm, fac_ref)))
+    ]
+    for copy in loads:
+        copy.start()
+
     barrier = pltpu.get_barrier_semaphore()
 
     def greet(pp, cc):
@@ -61,14 +70,6 @@
     for r in range(1, NY):
         greet(p, z * NY + lax.rem(y + r, NY))
 
-    loads = [
-        pltpu.make_async_copy(src, dst, sin.at[i])
-        for i, (src, dst) in enumerate((
-            (id_hbm, id_ref), (not_hbm, term_in.at[0]), (str_hbm, term_in.at[1]),
-            (cur_hbm, term_in.at[2]), (load_hbm, desc.at[0:F, :]), (fac_hbm, fac_ref)))
-    ]
-    for copy in loads:
-        copy.start()
     loads[0].wait()
 
     ids = id_ref[...]
@@ -314,11 +315,11 @@
     relay(1, 2)
     relay(2, 1)
     side_relay(2)
+    relay(3, 0)
     side_wait(0, 2)
     for d in (0, 1, 2):
         dots(d, 0)
     relay(2, 2)
-    relay(3, 0)
     dots(3, 0)
     side_wait(1, 2)
     for d in (0, 1, 2):

time: 60 us -> 59.8 us (level)
  no operation moved by 1% of the time
where the time goes in v10:
time: 59.8 us; the launch traced here: 59.6 us
  Pallas kernels  59 us (99%)
  between operations  0.64 us (1%)
    pallas_call x1, Pallas kernels, on_device(): pl.pallas_call(kernel, out_shape=(jax.ShapeDtypeStruct((paths, CP), BF),...  57.1 us
    pallas_call x1, Pallas kernels, on_device(): pl.pallas_call(hand_out, out_shape=tuple((jax.ShapeDtypeStruct(*s) for s...  1.9 us

profile of v10, /device:TPU:4, one launch (start us, length us, event | category | flops | bytes accessed | tf_op | source)
XLA Modules:
  0.0 59.6 jit_solution(14917451754514030613)
XLA Ops:
  0.6 57.1 %shard_map.77 = (bf16[1536,128]{1,0:T(8,128)(2,1)}, f32[4,128,128]{2,1,0:T(8,128)}) custom-call(bf16[64,1536]{1,0:T(8,128)(2,1)} %fac_hbm.1, bf16[64,2048]{1,0:T(8,128)(2,1)} %load_hbm.1, bf16[16,128]{1,0:T(8,128)(2,1)} %bitcast.6, bf16[16,128]{1,0:T(8,128)(2,1)} %bitcast.7, bf16[16,128]{1,0:T(8,128)(2,1)} %bitcast.8, s32[1,2048]{1,0:T(1,128)} %bitcast.5), custom_call_target="tpu_custom_call" | custom-call | tf_op jit(solution)/shard_map/pallas_call | solution.py:402
  57.7 1.9 %shard_map.78 = (bf16[1536,128]{1,0:T(8,128)(2,1)}, f32[4,128,128]{2,1,0:T(8,128)}) custom-call(bf16[1536,128]{1,0:T(8,128)(2,1)} %get-tuple-element.6.exp_in, f32[4,128,128]{2,1,0:T(8,128)} %get-tuple-element.7.mom_in), custom_call_target="tpu_custom_call" | custom-call | tf_op jit(solution)/shard_map/pallas_call | solution.py:439

commit v11 on v10

--- a/solution.py
+++ b/solution.py
@@ -87,7 +87,7 @@
         ranks.append(jnp.sum(part * before, axis=0, keepdims=True))
     rank = jnp.concatenate(ranks, axis=1).astype(jnp.int32)
     mine = lax.rem(owner + c, NQ) == quarter
-    code = jnp.where(mine, (owner // NQ) * SLOT + rank, -1)
+    code = jnp.where(mine, lax.rem(owner // NQ + 6 + NZ - z, NZ) * SLOT + rank, -1)
     for copy in loads[1:5]:
         copy.wait()
     line = lax.broadcasted_iota(jnp.int32, (ROWS - F, count), 0)
@@ -97,31 +97,39 @@
         flat = jnp.concatenate([cells[k:k + 1, :] for k in range(count // CP)], axis=1)
         extra = jnp.where(line == i, flat, extra)
     desc[F:ROWS, :] = extra.astype(BF)
-    total = jnp.zeros((ROWS, PER * SLOT), F32)
-    step = 512
-    for b in range(count // step):
-        cols = slice(b * step, (b + 1) * step)
-        chosen = (lax.broadcasted_iota(jnp.int32, (PER * SLOT, step), 0) == code[:, cols]).astype(F32).astype(BF)
-        total = total + lax.dot_general(desc[:, cols], chosen, NT, preferred_element_type=F32)
-    for i in range(PER):
-        pack[i] = total[:, i * SLOT:(i + 1) * SLOT].astype(BF)
-
+    place = c // NQ
+
+    def fill(group):
+        step, wide = 512, PER // 2
+        total = jnp.zeros((ROWS, wide * SLOT), F32)
+        for b in range(count // step):
+            cols = slice(b * step, (b + 1) * step)
+            slots = lax.broadcasted_iota(jnp.int32, (wide * SLOT, step), 0) + group * wide * SLOT
+            chosen = (slots == code[:, cols]).astype(F32).astype(BF)
+            total = total + lax.dot_general(desc[:, cols], chosen, NT, preferred_element_type=F32)
+        for i in range(wide):
+            pack[group * wide + i] = total[:, i * SLOT:(i + 1) * SLOT].astype(BF)
+
+    def hand_over(g):
+        to = first + NQ * lax.rem(z + g + 2, NZ)
+        return remote(pack.at[g], trades.at[quarter, place], s1.at[g], r1.at[place], p, to)
+
+    fill(0)
     pl.semaphore_wait(barrier, NP - 1 + 2 + NY - 1 + PER - (lax.rem(2 * c, NQ) == quarter).astype(jnp.int32))
-
-    place = c // NQ
-    for offset in (4, 3, 5, 2, 6, 1, 7, 0):
-        i = lax.rem(z + offset, PER)
-        copy = remote(pack.at[i], trades.at[quarter, place], s1.at[i], r1.at[place], p, first + NQ * i)
-        if offset:
-            copy.start()
-        else:
-            @pl.when(first != y)
-            def _(copy=copy):
-                copy.start()
-
-            @pl.when(first == y)
-            def _(i=i):
-                trades[quarter, place] = pack[i]
+    for g in (2, 1, 3, 0):
+        hand_over(g).start()
+    fill(1)
+    for g in (4, 5, 7):
+        hand_over(g).start()
+
+    @pl.when(first != y)
+    def _():
+        hand_over(6).start()
+
+    @pl.when(first == y)
+    def _():
+        trades[quarter, place] = pack[6]
+
     loads[5].wait()
     ft[...] = jnp.transpose(fac_ref[...].astype(F32)).astype(BF)
     for i, k in enumerate(targets):
@@ -315,11 +323,11 @@
     relay(1, 2)
     relay(2, 1)
     side_relay(2)
-    relay(3, 0)
     side_wait(0, 2)
     for d in (0, 1, 2):
         dots(d, 0)
     relay(2, 2)
+    relay(3, 0)
     dots(3, 0)
     side_wait(1, 2)
     for d in (0, 1, 2):
@@ -363,12 +371,13 @@
 
     for j in range(CH):
         out(j).wait()
-    for i, k in enumerate(targets):
-        copy = remote(pack.at[i], trades.at[quarter, place], s1.at[i], r1.at[place], p, k)
-
-        @pl.when(k != c)
-        def _(copy=copy):
-            copy.wait_send()
+    for g in (0, 1, 2, 3, 4, 5, 7):
+        hand_over(g).wait_send()
+
+    @pl.when(first != y)
+    def _():
+        hand_over(6).wait_send()
+
     for copy in sends:
         copy.wait_send()
     for d in range(FAR + 1):

time: 59.8 us -> 60 us (level)
  no operation moved by 1% of the time
where the time goes in v11:
time: 60 us; the launch traced here: 59.9 us
  Pallas kernels  59.3 us (99%)
  between operations  0.64 us (1%)
    pallas_call x1, Pallas kernels, on_device(): pl.pallas_call(kernel, out_shape=(jax.ShapeDtypeStruct((paths, CP), BF),...  57.4 us
    pallas_call x1, Pallas kernels, on_device(): pl.pallas_call(hand_out, out_shape=tuple((jax.ShapeDtypeStruct(*s) for s...  1.9 us

profile of v11, /device:TPU:4, one launch (start us, length us, event | category | flops | bytes accessed | tf_op | source)
XLA Modules:
  0.0 59.9 jit_solution(1717132756818232997)
XLA Ops:
  0.6 57.4 %shard_map.77 = (bf16[1536,128]{1,0:T(8,128)(2,1)}, f32[4,128,128]{2,1,0:T(8,128)}) custom-call(bf16[64,1536]{1,0:T(8,128)(2,1)} %fac_hbm.1, bf16[64,2048]{1,0:T(8,128)(2,1)} %load_hbm.1, bf16[16,128]{1,0:T(8,128)(2,1)} %bitcast.6, bf16[16,128]{1,0:T(8,128)(2,1)} %bitcast.7, bf16[16,128]{1,0:T(8,128)(2,1)} %bitcast.8, s32[1,2048]{1,0:T(1,128)} %bitcast.5), custom_call_target="tpu_custom_call" | custom-call | tf_op jit(solution)/shard_map/pallas_call | solution.py:411
  58.0 1.9 %shard_map.78 = (bf16[1536,128]{1,0:T(8,128)(2,1)}, f32[4,128,128]{2,1,0:T(8,128)}) custom-call(bf16[1536,128]{1,0:T(8,128)(2,1)} %get-tuple-element.6.exp_in, f32[4,128,128]{2,1,0:T(8,128)} %get-tuple-element.7.mom_in), custom_call_target="tpu_custom_call" | custom-call | tf_op jit(solution)/shard_map/pallas_call | solution.py:448

commit v12 on v10

--- a/solution.py
+++ b/solution.py
@@ -315,11 +315,11 @@
     relay(1, 2)
     relay(2, 1)
     side_relay(2)
-    relay(3, 0)
     side_wait(0, 2)
     for d in (0, 1, 2):
         dots(d, 0)
     relay(2, 2)
+    relay(3, 0)
     dots(3, 0)
     side_wait(1, 2)
     for d in (0, 1, 2):
@@ -334,9 +334,10 @@
         dots(3, j)
     ship(3)
     far(0)
+    pass_on(0)
+    pass_on(1)
     far(1)
-    for d in (0, 1, 2):
-        pass_on(d)
+    pass_on(2)
     far(2)
     ship(FAR)
     for d in (3, 0, 1, 2, FAR):

time: 59.8 us -> 59.5 us (level)
  no operation moved by 1% of the time
where the time goes in v12:
time: 59.5 us; the launch traced here: 59.4 us
  Pallas kernels  58.7 us (99%)
  between operations  0.64 us (1%)
    pallas_call x1, Pallas kernels, on_device(): pl.pallas_call(kernel, out_shape=(jax.ShapeDtypeStruct((paths, CP), BF),...  56.8 us
    pallas_call x1, Pallas kernels, on_device(): pl.pallas_call(hand_out, out_shape=tuple((jax.ShapeDtypeStruct(*s) for s...  1.9 us

profile of v12, /device:TPU:4, one launch (start us, length us, event | category | flops | bytes accessed | tf_op | source)
XLA Modules:
  0.0 59.4 jit_solution(4995150684202772841)
XLA Ops:
  0.6 56.8 %shard_map.77 = (bf16[1536,128]{1,0:T(8,128)(2,1)}, f32[4,128,128]{2,1,0:T(8,128)}) custom-call(bf16[64,1536]{1,0:T(8,128)(2,1)} %fac_hbm.1, bf16[64,2048]{1,0:T(8,128)(2,1)} %load_hbm.1, bf16[16,128]{1,0:T(8,128)(2,1)} %bitcast.6, bf16[16,128]{1,0:T(8,128)(2,1)} %bitcast.7, bf16[16,128]{1,0:T(8,128)(2,1)} %bitcast.8, s32[1,2048]{1,0:T(1,128)} %bitcast.5), custom_call_target="tpu_custom_call" | custom-call | tf_op jit(solution)/shard_map/pallas_call | solution.py:403
  57.5 1.9 %shard_map.78 = (bf16[1536,128]{1,0:T(8,128)(2,1)}, f32[4,128,128]{2,1,0:T(8,128)}) custom-call(bf16[1536,128]{1,0:T(8,128)(2,1)} %get-tuple-element.6.exp_in, f32[4,128,128]{2,1,0:T(8,128)} %get-tuple-element.7.mom_in), custom_call_target="tpu_custom_call" | custom-call | tf_op jit(solution)/shard_map/pallas_call | solution.py:440
